TPU v7x, 512 devices: a whole 4x8x8 slice. The times are simulated.
512 devices in a mesh: gx: 8 (over z), gy: 8 (over y), gz: 8 (over x, core).
Axes of the slice: x: 4, y: 8, z: 8, core: 2. Of those that a mesh axis runs over, the one named last changes fastest.
Arguments:
- right_side: float32 [512, 512, 512], P('gx', 'gy', 'gz'), may hold values from -6 to 6
- guess: float32 [512, 512, 512], P('gx', 'gy', 'gz'), may hold values from -6 to 6
Outputs:
- solution: float32 [512, 512, 512], P('gx', 'gy', 'gz')
- residual: float32 [512, 512, 512], P('gx', 'gy', 'gz')
All inputs are finite; a program needn't handle non-finite values.
Results may differ from a plain program's by a relative error of at most 0.0003.
Values sent between devices are 32-bit elements.
A program may use at most 256 MiB of HBM per device.

v0:
```python
import jax
import jax.numpy as jnp
from jax import lax
from jax.sharding import PartitionSpec as P

LEVELS = 7
COARSE_SWEEPS = 4


def padded_2(value, sides, width, wrap):
    for axis, dim in sides:
        count, length = lax.axis_size(axis), value.shape[dim]
        up = [(i, (i + 1) % count) for i in range(count if wrap else count - 1)]
        down = [(j, i) for i, j in up]
        last = lax.slice_in_dim(value, length - width, length, axis=dim)
        leading = lax.slice_in_dim(value, 0, width, axis=dim)
        before = lax.ppermute(last, axis, up)
        after = lax.ppermute(leading, axis, down)
        value = jnp.concatenate([before, value, after], axis=dim)
    return value


def face_total(padded):
    total = padded[2:, 1:-1, 1:-1] + padded[:-2, 1:-1, 1:-1]
    total = total + padded[1:-1, 2:, 1:-1] + padded[1:-1, :-2, 1:-1]
    total = total + padded[1:-1, 1:-1, 2:] + padded[1:-1, 1:-1, :-2]
    return total


def walls(index, total):
    return (index == 0).astype(jnp.float32) + (index == total - 1).astype(jnp.float32)


def frame(offsets, block, totals):
    first = (offsets[0] + lax.iota(jnp.int32, block[0]))[:, None, None]
    second = (offsets[1] + lax.iota(jnp.int32, block[1]))[None, :, None]
    third = (offsets[2] + lax.iota(jnp.int32, block[2]))[None, None, :]
    parity = (first + second + third) % 2
    diagonal = 6.0 + walls(first, totals[0]) + walls(second, totals[1]) + walls(third, totals[2])
    return (parity == 0, parity == 1, diagonal)


def level_frame(places, counts, size):
    offsets = tuple((place * size for place in places))
    totals = tuple((count * size for count in counts))
    return frame(offsets, (size, size, size), totals)


def relax(padded, source, colour, diagonal, scale):
    updated = (scale * source + face_total(padded)) / diagonal
    return jnp.where(colour, updated, padded[1:-1, 1:-1, 1:-1])


def residual_on(padded, source, diagonal, inverse):
    return source - (diagonal * padded[1:-1, 1:-1, 1:-1] - face_total(padded)) * inverse


def restrict(remainder):
    shape = remainder.shape
    grouped = remainder.reshape(shape[0] // 2, 2, shape[1] // 2, 2, shape[2] // 2, 2)
    return jnp.sum(grouped, axis=(1, 3, 5)) * 0.125


def odd_pad(field):
    for axis in range(3):
        count = field.shape[axis]
        lowest = -lax.slice_in_dim(field, 0, 1, axis=axis)
        highest = -lax.slice_in_dim(field, count - 1, count, axis=axis)
        field = jnp.concatenate([lowest, field, highest], axis=axis)
    return field


def prolong(padded):
    centre = padded[1:-1, 1:-1, 1:-1]
    below_first = 0.25 * (padded[:-2, 1:-1, 1:-1] - centre)
    above_first = 0.25 * (padded[2:, 1:-1, 1:-1] - centre)
    below_second = 0.25 * (padded[1:-1, :-2, 1:-1] - centre)
    above_second = 0.25 * (padded[1:-1, 2:, 1:-1] - centre)
    below_third = 0.25 * (padded[1:-1, 1:-1, :-2] - centre)
    above_third = 0.25 * (padded[1:-1, 1:-1, 2:] - centre)
    along_first = jnp.stack([below_first, above_first], axis=1)[:, :, :, None, :, None]
    along_second = jnp.stack([below_second, above_second], axis=2)[:, None, :, :, :, None]
    along_third = jnp.stack([below_third, above_third], axis=3)[:, None, :, None, :, :]
    fine = centre[:, None, :, None, :, None] + along_first + along_second + along_third
    shape = centre.shape
    return fine.reshape(2 * shape[0], 2 * shape[1], 2 * shape[2])


def down_halo(field):
    return padded_2(field, (("gx", 0), ("gy", 1), ("gz", 2)), 1, False)


def up_halo(field):
    return padded_2(field, (("gx", 0), ("gy", 1), ("gz", 2)), 1, False)


def lift_halo(field):
    return padded_2(field, (("gx", 0), ("gy", 1), ("gz", 2)), 1, False)


def pad_zero(field):
    return jnp.pad(field, 1)


def reflect(padded, axis, lowest, highest):
    moved = jnp.moveaxis(padded, axis, 0)
    moved = moved.at[0].set(jnp.where(lowest, -moved[1], moved[0]))
    moved = moved.at[-1].set(jnp.where(highest, -moved[-2], moved[-1]))
    return jnp.moveaxis(moved, 0, axis)


def reflect_all(padded, places, counts):
    for axis in range(3):
        padded = reflect(padded, axis, places[axis] == 0, places[axis] == counts[axis] - 1)
    return padded


def descend(field, source, level, geometry):
    red, black, diagonal = geometry
    scale = 4.0**level
    if level == 0:
        first = relax(down_halo(field), source, red, diagonal, scale)
    else:
        first = jnp.where(red, scale * source / diagonal, 0.0)
    second = relax(down_halo(first), source, black, diagonal, scale)
    remainder = residual_on(down_halo(second), source, diagonal, 0.25**level)
    return (second, restrict(remainder))


def ascend(smoothed, source, padded, level, geometry):
    red, black, diagonal = geometry
    scale = 4.0**level
    fine = smoothed + prolong(padded)
    first = relax(up_halo(fine), source, red, diagonal, scale)
    return relax(up_halo(first), source, black, diagonal, scale)


def bottom_sweeps(source, geometry, scale, widen):
    red, black, diagonal = geometry
    field = jnp.where(red, scale * source / diagonal, 0.0)
    field = relax(widen(field), source, black, diagonal, scale)
    for sweep_index in range(COARSE_SWEEPS - 1):
        field = relax(widen(field), source, red, diagonal, scale)
        field = relax(widen(field), source, black, diagonal, scale)
    return field


def collect(source, counts):
    block = source.shape
    whole = lax.all_gather(source.reshape(1, -1), ("gx", "gy", "gz"), axis=0, tiled=True)
    grid = whole.reshape(counts + block)
    grid = jnp.transpose(grid, (0, 3, 1, 4, 2, 5))
    return grid.reshape(counts[0] * block[0], counts[1] * block[1], counts[2] * block[2])


def bottom(source, places, counts):
    scale = 4.0 ** (LEVELS - 1)
    size = source.shape[0]
    whole = collect(source, counts)
    correction = bottom_sweeps(whole, frame((0, 0, 0), whole.shape, whole.shape), scale, pad_zero)
    starts = (places[0] * size, places[1] * size, places[2] * size)
    padded = lax.dynamic_slice(odd_pad(correction), starts, (size + 2, size + 2, size + 2))
    return padded


def per_device(right_side, guess):
    counts = (lax.axis_size("gx"), lax.axis_size("gy"), lax.axis_size("gz"))
    places = (lax.axis_index("gx"), lax.axis_index("gy"), lax.axis_index("gz"))
    block = right_side.shape[0]
    frames = [level_frame(places, counts, block >> level) for level in range(LEVELS - 1)]
    field = guess
    source = right_side
    sources = []
    kept = []
    for level in range(LEVELS - 1):
        smoothed, coarse = descend(field, source, level, frames[level])
        sources.append(source)
        kept.append(smoothed)
        field = coarse
        source = coarse
    padded = bottom(source, places, counts)
    fine = guess
    for level in reversed(range(LEVELS - 1)):
        fine = ascend(kept[level], sources[level], padded, level, frames[level])
        if level > 0:
            padded = reflect_all(lift_halo(fine), places, counts)
    red, black, diagonal = frames[0]
    return (fine, residual_on(up_halo(fine), right_side, diagonal, 1.0))


def solution(mesh):
    return jax.shard_map(
        per_device,
        mesh=mesh,
        in_specs=(P("gx", "gy", "gz"), P("gx", "gy", "gz")),
        out_specs=(P("gx", "gy", "gz"), P("gx", "gy", "gz")),
        check_vma=False,
    )
```

profile of v0, /device:TPU:1, one launch (start us, length us, event | category | flops | bytes accessed | tf_op | source)
XLA Modules:
  0.0 1409.0 jit_solution(637733215440395271)
XLA Ops:
  27.3 6.0 collective-permute-start.5
  43.2 11.7 fusion.1
  96.9 13.8 fusion.2
  157.2 15.9 %fusion.4 = f32[64,64,64]{2,1,0:T(8,128)} fusion(f32[64,64,64]{2,1,0:T(8,128)S(1)} %copy-done, f32[64,64,64]{2,1,0:T(8,128)} %copy-done.1, f32[66,66,1]{2,1,0:T(8,128)} %copy.290, f32[66,1,64]{2,1,0:T(1,128)S(1)} %collective-permute-done.14, f32[66,1,64]{2,1,0:T(1,128)S(1)} %collective-permute-done.15, f32[1,64,64]{2,1,0:T(8,128)S(1)} %collective-permute-done.12, ...), kind=kLoop, calls=%fused_computation.23 | loop fusion | flops 7077888 | bytes 3263776 | tf_op jit(solution)/shard_map/sub | solution.py:55
  173.2 71.5 %reshape.1848 = f32[32,2,32,2,32,2]{5,4,3,2,1,0:T(8,128)} reshape(f32[64,64,64]{2,1,0:T(8,128)} %fusion.4) | data formatting | bytes 2097152 | tf_op jit(solution)/shard_map/reshape | solution.py:60
  244.6 20.8 %reduce_sum.54 = f32[32,32,32]{2,1,0:T(8,128)S(1)} reduce(f32[32,2,32,2,32,2]{5,4,3,2,1,0:T(8,128)} %reshape.1848, f32[]{:T(128)} %constant.823.clone.1), dimensions={1,3,5}, to_apply=%region_0.1 | reduce | flops 229376 | bytes 1179652 | tf_op jit(solution)/shard_map/reduce_sum | solution.py:61
  339.9 7.1 reshape.1849
  395.1 7.4 collective-permute-start.41
  427.1 7.3 collective-permute-start.47
  454.2 7.3 collective-permute-start.53
  483.7 7.3 collective-permute-start.59
  510.1 7.2 collective-permute-start.65
  536.7 7.2 collective-permute-start.71
  561.9 7.1 collective-permute-start.77
  571.8 94.9 %all-reduce.7 = f32[512]{0:T(512)S(1)} all-reduce(f32[512]{0:T(512)S(1)} %dynamic-update-slice.90), channel_id=1, replica_groups=mesh['gx'=8,'gy'=8,'gz'=8] {'gx','gy','gz'}, use_global_device_ids=true, to_apply=%add.7 | all-reduce | flops 512 | bytes 4096
  749.7 6.5 collective-permute-start.94
  826.6 7.1 collective-permute-start.112
  887.5 6.4 collective-permute-start.125
  910.7 7.1 collective-permute-start.130
  978.1 7.3 collective-permute-start.143
  1003.3 7.3 collective-permute-start.148
  1031.2 6.4 broadcast_add_fusion.1
  1037.6 7.1 add.2485
  1099.2 5.8 collective-permute-start.161
  1128.2 6.6 collective-permute-start.166
  1149.3 7.2 scatter.149
  1160.5 9.3 copy.325
  1172.6 27.0 %broadcast_add_fusion = f32[32,2,32,2,32,2]{5,4,3,2,1,0:T(8,128)} fusion(f32[32,32,32,2]{3,2,1,0:T(8,128)} %copy.325, f32[32,2,32,2,32]{4,3,2,1,0:T(2,128)S(1)} %broadcast_add_fusion.2), kind=kLoop, calls=%fused_computation | loop fusion | flops 262144 | bytes 1835008 | tf_op jit(solution)/shard_map/add | solution.py:84
  1199.6 54.9 %add.2507 = f32[64,64,64]{2,1,0:T(8,128)} reshape(f32[32,2,32,2,32,2]{5,4,3,2,1,0:T(8,128)} %broadcast_add_fusion) | data formatting | bytes 2097152 | tf_op jit(solution)/shard_map/add | solution.py:84
  1292.5 13.8 fusion.5
  1342.0 13.8 fusion.6
  1392.0 16.4 %fusion.8 = f32[64,64,64]{2,1,0:T(8,128)} fusion(f32[64,64,64]{2,1,0:T(8,128)S(1)} %copy-done, f32[64,64,64]{2,1,0:T(8,128)} %copy-done.3, f32[66,66,1]{2,1,0:T(8,128)} %copy.337, f32[66,1,64]{2,1,0:T(1,128)S(1)} %collective-permute-done.182, f32[66,1,64]{2,1,0:T(1,128)S(1)} %collective-permute-done.183, f32[1,64,64]{2,1,0:T(8,128)S(1)} %collective-permute-done.180, ...), kind=kLoop, calls=%fused_computation.27 | loop fusion | flops 7077888 | bytes 3263776 | tf_op jit(solution)/shard_map/sub | solution.py:55
  (840 shorter events, 893.8 us)
Async XLA Ops:
  1.4 9.5 collective-permute-start
  27.3 13.6 collective-permute-start.5
  82.8 11.8 collective-permute-start.11
  143.1 11.8 collective-permute-start.17
  288.0 10.8 collective-permute-start.23
  324.7 11.1 collective-permute-start.29
  366.7 8.7 collective-permute-start.34
  393.2 11.0 collective-permute-start.40
  395.1 10.2 collective-permute-start.41
  425.2 9.7 collective-permute-start.46
  427.1 9.0 collective-permute-start.47
  452.3 9.7 collective-permute-start.52
  454.2 8.9 collective-permute-start.53
  481.8 9.2 collective-permute-start.58
  508.2 9.1 collective-permute-start.64
  534.8 9.1 collective-permute-start.70
  559.9 9.0 collective-permute-start.76
  697.1 8.6 collective-permute-start.82
  721.2 8.8 collective-permute-start.88
  749.7 8.8 collective-permute-start.94
  801.4 9.0 collective-permute-start.106
  826.6 9.0 collective-permute-start.112
  885.1 9.0 collective-permute-start.124
  910.7 9.1 collective-permute-start.130
  976.2 10.9 collective-permute-start.142
  978.1 10.1 collective-permute-start.143
  1003.3 10.1 collective-permute-start.148
  1095.5 9.5 collective-permute-start.160
  1128.2 8.9 collective-permute-start.166
  1278.6 9.2 collective-permute-start.172
  1327.4 9.9 collective-permute-start.178
  1376.9 10.5 collective-permute-start.184
  (209 other events, 4022.0 us)
where the time goes:
time: 1430 us; the launch traced here: 1410 us
  starting transfers between devices  523 us (37%)
  local copies, waits for them, and re-layouts  304 us (21%)
  waiting for transfers between devices  248 us (17%)
  other arithmetic  226 us (16%)
  blocking collectives  94.9 us (7%)
    ppermute x93, starting transfers between devices, padded_2(): before = lax.ppermute(last, axis, up)  367 us
    ppermute x93, waiting for transfers between devices, padded_2(): after = lax.ppermute(leading, axis, down)  231 us
    ppermute x93, starting transfers between devices, padded_2(): after = lax.ppermute(leading, axis, down)  156 us
    unnamed x1, blocking collectives  94.9 us
    reshape x5, local copies, waits for them, and re-layouts, restrict(): remainder.reshape(shape[0] // 2, 2, shape[1] // 2, 2, shape[2] // 2, 2)  81.6 us
    select_n x26, other arithmetic, relax(): return jnp.where(colour, updated, padded[1:-1, 1:-1, 1:-1])  81 us
    add x5, local copies, waits for them, and re-layouts, prolong(): centre[:, None, :, None, :, None] + along_first + along_second + along_third  65.3 us
    slice x38, local copies, waits for them, and re-layouts, padded_2(): leading = lax.slice_in_dim(value, 0, width, axis=dim)  49.4 us
  transfers between devices with their start and end apart: 186, of which 96 were waited for; matrix products, arithmetic and copies ran while one was open for 3% of the time, Pallas kernels for 0%

commit v1 on v0

v1 whole, which is shorter than its diff:
```python
import itertools

import jax
import jax.numpy as jnp
from jax import lax
from jax.experimental import pallas as pl
from jax.experimental.pallas import tpu as pltpu
from jax.sharding import PartitionSpec as P

COARSE_SWEEPS = 4
MESH = pl.DeviceIdType.MESH
SIDE = 8
F32 = jnp.float32


class Level:
    def __init__(self, n, total, po, oy, p0, np_, r0, nr, pairs, rows, whole_z):
        self.n, self.total, self.po, self.oy = n, total, po, oy
        self.p0, self.np, self.r0, self.nr = p0, np_, r0, nr
        self.pairs, self.rows, self.whole_z = pairs, rows, whole_z

    def shape(self):
        return (self.pairs, self.rows, 128)


LEV = [
    Level(64, 512, 3, 8, 1, 36, 4, 72, 38, 80, False),
    Level(32, 256, 5, 16, 1, 24, 8, 48, 26, 64, False),
    Level(16, 128, 5, 16, 1, 16, 8, 32, 18, 48, False),
    Level(8, 64, 5, 16, 1, 12, 8, 24, 14, 40, True),
    Level(32, 32, 4, 8, 4, 16, 8, 32, 24, 48, True),
    Level(16, 16, 1, 8, 1, 8, 8, 16, 10, 32, True),
    Level(8, 8, 1, 8, 1, 4, 8, 8, 6, 24, True),
]
GIVE = {0: (3, 20, 12, 40), 1: (2, 14, 12, 24), 2: (2, 10, 12, 16), 3: (0, 8, 0, 12), 4: (0, 10, 8, 16), 5: (0, 6, 8, 8)}
WIDTH = {1: 6, 2: 7}


def iota(shape, axis):
    return lax.broadcasted_iota(jnp.int32, shape, axis)


def odd(rows):
    return ((iota((rows, 128), 0) + iota((rows, 128), 1)) & 1) == 1


def lanes(rows):
    return iota((rows, 128), 1)


def sweep_loop(start, count, step, body):
    step = max(k for k in range(1, step + 1) if count % k == 0)
    if count == step:
        for i in range(count):
            body(start + i)
        return

    def some(j, carry):
        for i in range(step):
            body(start + j * step + i)
        return carry

    lax.fori_loop(0, count // step, some, 0)


def around(src, p, r0, nr, up):
    here = src[p, pl.ds(r0, nr), :]
    side = jnp.where(up, src[p + 1, pl.ds(r0, nr), :], src[p - 1, pl.ds(r0, nr), :])
    rows = src[p, pl.ds(r0 - 1, nr), :] + src[p, pl.ds(r0 + 1, nr), :]
    return (here + side) + rows + (pltpu.roll(here, 1, axis=1) + pltpu.roll(here, 127, axis=1))


def kernel(*refs):
    it = iter(refs)
    f_hbm, u_hbm, out_u, out_r = (next(it) for _ in range(4))
    f_in, u_in = next(it), next(it)
    R = [next(it) for _ in range(7)]
    B = [next(it) for _ in range(7)]
    FR = [next(it) for _ in range(7)]
    FB = [next(it) for _ in range(7)]
    C = [next(it) for _ in range(7)]
    D = [next(it) for _ in range(7)]
    A = [next(it) for _ in range(6)]
    Q = [next(it) for _ in range(6)]
    EX = [next(it) for _ in range(6)]
    EZ = [next(it) for _ in range(6)]
    T, H = next(it), next(it)
    G = {1: next(it), 2: next(it)}
    N = {5: next(it), 6: next(it)}
    zs = {k: (next(it), next(it)) for k in ("f", "v", 1, 2)}
    zr = {k: (next(it), next(it)) for k in ("f", "v", 1, 2)}
    pack3, Z3, pack4, G4, A4 = (next(it) for _ in range(5))
    sems = {k: (next(it), next(it)) for k in ("f", "v", 1, 2, "3", "4")}
    in_sem, out_sem = next(it), next(it)

    gx, gy, gz = lax.axis_index("gx"), lax.axis_index("gy"), lax.axis_index("gz")
    me = (gx, gy, gz)

    copies_in = []
    for i, (src, dst) in enumerate(((u_hbm, u_in), (f_hbm, f_in))):
        copy = pltpu.make_async_copy(src, dst, in_sem.at[i])
        copy.start()
        copies_in.append(copy)

    barrier = pltpu.get_barrier_semaphore()
    count = jnp.int32(0)
    for dx, dy in itertools.product((-1, 0, 1), repeat=2):
        there = inside((dx, dy, 0), me)

        def column(k, carry, dx=dx, dy=dy):
            @pl.when(k != gz)
            def _():
                pl.semaphore_signal(barrier, inc=1, device_id=(gx + dx, gy + dy, k), device_id_type=MESH)

            return carry

        @pl.when(there)
        def _():
            lax.fori_loop(0, SIDE, column, 0)

        count = count + jnp.where(there, SIDE - 1, 0)

    def plane(k, carry):
        x, y = k // SIDE, k % SIDE

        @pl.when((x != gx) | (y != gy))
        def _():
            pl.semaphore_signal(barrier, inc=1, device_id=(x, y, gz), device_id_type=MESH)

        return carry

    lax.fori_loop(0, SIDE * SIDE, plane, 0)
    pl.semaphore_wait(barrier, count + SIDE * SIDE - 1)

    lv = LEV[0]
    m64 = ((iota((64, 64), 0) + iota((64, 64), 1)) & 1) == 1
    for copy in copies_in:
        copy.wait()

    def apart(p):
        a, b = u_in[2 * (p - lv.po)], u_in[2 * (p - lv.po) + 1]
        B[0][p, 8:72, 0:64] = jnp.where(m64, a, b)
        a, b = f_in[2 * (p - lv.po)], f_in[2 * (p - lv.po) + 1]
        FR[0][p, 8:72, 0:64] = jnp.where(m64, b, a)
        FB[0][p, 8:72, 0:64] = jnp.where(m64, a, b)

    sweep_loop(3, 32, 8, apart)

    lane64 = lanes(64)

    def pack_first(get, keys, slots, low, high, width):
        for g in range(slots // 16):
            lo = hi = None
            for j in range(16):
                t = get(16 * g + j)
                t = pltpu.roll(t, 8 * j, axis=1) if j else t
                rows = t.shape[0]
                lane = lanes(rows)
                if lo is None:
                    lo, hi = t, t
                else:
                    lo = jnp.where(((lane - 8 * j) & 127) < width, t, lo)
                    hi = jnp.where(((lane - high - 8 * j) & 127) < width, t, hi)
            keys[0][g] = lo
            keys[1][g] = hi

    def face_first(i):
        b = B[0][3 + i, 8:72, :]
        r = pltpu.roll(FR[0][3 + i, 8:72, :], 3, axis=1)
        k = pltpu.roll(FB[0][3 + i, 8:72, :], 5, axis=1)
        t = jnp.where((lane64 == 5) | (lane64 == 68), k, b)
        return jnp.where((lane64 == 3) | (lane64 == 4) | (lane64 == 65) | (lane64 == 66), r, t)

    pack_first(face_first, zs["f"], 32, 0, 61, 8)

    def exchange(key, arrays, po, own, oy, n, hz):
        send, recv = sems[key]
        groups = zs[key][0].shape[0]
        waits = []
        at = 0
        for d in sorted(itertools.product((-1, 0, 1), repeat=3), key=lambda d: -sum(map(abs, d))):
            if d == (0, 0, 0):
                continue
            dx, dy, dz = d
            device = (gx + dx, gy + dy, gz + dz)
            pieces = []
            if dz == 0:
                for src_ref, dst_ref, hp, hr in arrays:
                    ps, pd, pw = {-1: (po, po + own, hp), 0: (po, po, own), 1: (po + own - hp, po - hp, hp)}[dx]
                    rs, rd, rw = {-1: (oy, oy + n, hr), 0: (oy, oy, n), 1: (oy + n - hr, oy - hr, hr)}[dy]
                    pieces.append((src_ref.at[pl.ds(ps, pw), pl.ds(rs, rw), :], dst_ref.at[pl.ds(pd, pw), pl.ds(rd, rw), :]))
            else:
                hr = hz
                qs, qd, qw = {-1: (0, groups + 1, 1), 0: (0, 1, groups), 1: (groups - 1, 0, 1)}[dx]
                rs, rd, rw = {-1: (0, oy + n, hr), 0: (0, oy, n), 1: (n - hr, oy - hr, hr)}[dy]
                src_ref, dst_ref = (zs[key][0], zr[key][1]) if dz < 0 else (zs[key][1], zr[key][0])
                pieces.append((src_ref.at[pl.ds(qs, qw), pl.ds(rs, rw), :], dst_ref.at[pl.ds(qd, qw), pl.ds(rd, rw), :]))
            copies = []
            for src, dst in pieces:
                copies.append(pltpu.make_async_remote_copy(src, dst, send.at[at], recv.at[at], device_id=device, device_id_type=MESH))
                at += 1
            to, source = inside(d, me), inside((-dx, -dy, -dz), me)

            @pl.when(to)
            def _(copies=copies):
                for copy in copies:
                    copy.start()

            waits.append((to, source, copies))
        return waits

    def wait_recv(waits):
        for _, source, copies in waits:

            @pl.when(source)
            def _(copies=copies):
                for copy in copies:
                    copy.wait_recv()

    def wait_send(waits):
        for to, _, copies in waits:

            @pl.when(to)
            def _(copies=copies):
                for copy in copies:
                    copy.wait_send()

    first = exchange("f", ((B[0], B[0], 2, 3), (FR[0], FR[0], 1, 2), (FB[0], FB[0], 1, 1)), 3, 32, 8, 64, 3)

    def outside(ref, po, own, hp, oy, n, hr):
        planes, rows = ref.shape[0], ref.shape[1]
        for cond, cut in (
            (gx == 0, (slice(po - hp, po), slice(0, rows))),
            (gx == SIDE - 1, (slice(po + own, po + own + hp), slice(0, rows))),
            (gy == 0, (slice(0, planes), slice(oy - hr, oy))),
            (gy == SIDE - 1, (slice(0, planes), slice(oy + n, oy + n + hr))),
        ):

            @pl.when(cond)
            def _(cut=cut):
                shape = (cut[1].stop - cut[1].start, 128)
                for p in range(cut[0].start, cut[0].stop):
                    ref[p, cut[1], :] = jnp.zeros(shape, F32)

    def outside_z(key):
        for side, cond in ((0, gz == 0), (1, gz == SIDE - 1)):

            @pl.when(cond)
            def _(side=side):
                ref = zr[key][side]
                ref[...] = jnp.zeros(ref.shape, F32)

    def edges_z(key, po, n, hz, oy, groups):
        for side in (0, 1):
            ref = zr[key][side]
            rows = ref.shape[1]
            for cond, cut in (
                (gx == 0, (0, 1, 0, rows)),
                (gx == SIDE - 1, (groups + 1, 1, 0, rows)),
                (gy == 0, (0, groups + 2, oy - hz, hz)),
                (gy == SIDE - 1, (0, groups + 2, oy + n, hz)),
            ):

                @pl.when(cond)
                def _(cut=cut, ref=ref):
                    ref[pl.ds(cut[0], cut[1]), pl.ds(cut[2], cut[3]), :] = jnp.zeros((cut[1], cut[3], 128), F32)

    for ref, hp, hr in ((B[0], 2, 3), (FR[0], 1, 2), (FB[0], 1, 1), (H, 2, 3)):
        outside(ref, 3, 32, hp, 8, 64, hr)
    for key, n, oy, groups, hz in (("f", 64, 8, 2, 3), ("v", 64, 8, 2, 3), (1, 32, 16, 2, 6), (2, 16, 16, 1, 7)):
        outside_z(key)
        edges_z(key, 3, n, hz, oy, groups)
    outside(G[1], 8, 32, 8, 16, 32, 8)
    outside(G[2], 8, 16, 8, 16, 16, 8)
    for dx, dy in itertools.product((-1, 0, 1), repeat=2):
        if (dx, dy) != (0, 0):

            @pl.when(jnp.logical_not(inside((dx, dy, 0), me)))
            def _(dx=dx, dy=dy):
                Z3[dx + 1, dy + 1] = jnp.zeros((SIDE, 8, 128), F32)

    for l in (4, 5, 6):
        R[l][...] = jnp.zeros(LEV[l].shape(), F32)
        B[l][...] = jnp.zeros(LEV[l].shape(), F32)
    for l in (4, 5):
        EX[l][...] = jnp.zeros(EX[l].shape, F32)

    def tables(l):
        lv = LEV[l]
        shape = (lv.nr, 128)
        row, lane = iota(shape, 0) + lv.r0, iota(shape, 1)
        y = row - lv.oy
        z = jnp.where(lane < 100, lane, lane - 128)
        if l < 4:
            y = y + gy * lv.n
        if l < 3:
            z = z + gz * lv.n
        last = lv.total - 1
        within = (y >= 0) & (y <= last) & (z >= 0) & (z <= last)
        one = lambda c: jnp.where(c, 1, 0)
        w = one(y == 0) + one(y == last) + one(z == 0) + one(z == last)
        high = one(odd(lv.nr))
        for kind, colour in itertools.product(range(3), range(2)):
            a = high if colour == 0 else 1 - high
            d = w if kind == 0 else (w + 1 - a if kind == 1 else w + a)
            inv = jnp.where(d == 0, 1 / 6, jnp.where(d == 1, 1 / 7, jnp.where(d == 2, 1 / 8, 1 / 9)))
            C[l][kind, colour] = jnp.where(within, inv, 0.0)
            D[l][kind, colour] = 6.0 + d.astype(F32)
            if colour == 1 and l < 6:
                q = jnp.where(within, 0.25, 0.0)
                Q[l][kind] = q
                A[l][kind] = (1.0 - d.astype(F32)) * q
        for colour in range(2):
            C[l][3, colour] = jnp.zeros(shape, F32)
            D[l][3, colour] = jnp.full(shape, 6.0, F32)
        if l < 6:
            Q[l][3] = jnp.zeros(shape, F32)
            A[l][3] = jnp.zeros(shape, F32)

    for l in range(7):
        tables(l)

    def kind(l, p):
        lv = LEV[l]
        x = 2 * (p - lv.po) + (gx * lv.n if l < 4 else 0)
        if l >= 4:
            return jnp.where(x == 0, 1, jnp.where(x == lv.total - 2, 2, 0))
        return jnp.where(x == 0, 1, jnp.where(x == lv.total - 2, 2, jnp.where((x < 0) | (x >= lv.total), 3, 0)))

    wait_recv(first)
    wait_send(first)
    lane72 = lanes(72)

    def slot_of(i, n):
        groups = n // 16
        if i < 0:
            return 0, 16 + i
        if i >= n:
            return groups + 1, i - n
        return 1 + i // 16, i % 16

    def unpack_first(i, first_half):
        g, j = slot_of(i, 32)
        p = 3 + i
        low, high = zr["f"][0][g, 4:76, :], zr["f"][1][g, 4:76, :]
        for ref, at, width, shift in ((B[0], 0, 3, 64), (FR[0], 3, 2, 61), (FB[0], 5, 1, 59)):
            w = jnp.where(((lane72 - 8 * j - at) & 127) < width, high, low)
            w = pltpu.roll(w, (shift - 8 * j) % 128, axis=1)
            ref[p, 4:76, :] = jnp.where(lane72 < 64, ref[p, 4:76, :], w)

    for i in range(-2, 34):
        unpack_first(i, None)

    def red_sweep(l):
        lv = LEV[l]
        m = odd(lv.nr)

        def body(p):
            s = around(B[l], p, lv.r0, lv.nr, m)
            R[l][p, pl.ds(lv.r0, lv.nr), :] = (FR[l][p, pl.ds(lv.r0, lv.nr), :] + s) * C[l][kind(l, p), 0]

        sweep_loop(lv.p0, lv.np, 12, body)

    def black_sweep(l, keep):
        lv = LEV[l]
        m = jnp.logical_not(odd(lv.nr))

        def body(p):
            t = kind(l, p)
            rows = pl.ds(lv.r0, lv.nr)
            fs = FB[l][p, rows, :] + around(R[l], p, lv.r0, lv.nr, m)
            b = fs * C[l][t, 1]
            B[l][p, rows, :] = b
            if keep:
                T[p, rows, :] = fs - D[l][t, 1] * b

        sweep_loop(lv.p0, lv.np, 12, body)

    def red_residual(l, p):
        lv = LEV[l]
        s = around(B[l], p, lv.oy, lv.n, odd(lv.n))
        at = lv.oy - lv.r0
        return FR[l][p, pl.ds(lv.oy, lv.n), :] + s - D[l][kind(l, p), 0, pl.ds(at, lv.n), :] * R[l][p, pl.ds(lv.oy, lv.n), :]

    def coarse_side(l, p):
        lv = LEV[l]
        T[p, pl.ds(lv.oy, lv.n), :] = T[p, pl.ds(lv.oy, lv.n), :] + red_residual(l, p)
        half = lv.n // 2
        u = T[p, pl.ds(lv.oy, half, stride=2), :] + T[p, pl.ds(lv.oy + 1, half, stride=2), :]
        u = u + pltpu.roll(u, 127, axis=1)
        return 0.5 * jnp.take_along_axis(u, (2 * lanes(half)) & 127, axis=1, mode="promise_in_bounds")

    red_sweep(0)
    black_sweep(0, True)

    def keep_black(p):
        H[p, 8:72, :] = B[0][p, 8:72, :]

    sweep_loop(3, 32, 8, keep_black)

    def restrict_to(l, dst, first_plane, first_row):
        lv = LEV[l]

        def body(p):
            dst[p - lv.po + first_plane, pl.ds(first_row, lv.n // 2), :] = coarse_side(l, p)

        sweep_loop(lv.po, lv.n // 2, 8, body)

    restrict_to(0, G[1], 8, 16)

    def send_right_side(l):
        n, w = LEV[l].n, WIDTH[l]
        pack_first(lambda i: G[l][8 + i, pl.ds(16, n), :], zs[l], n, 0, n - 8, 8)
        return exchange(l, ((G[l], G[l], w, w),), 8, n, 16, n, w)

    def split_right_side(l):
        lv = LEV[l]
        n = lv.n
        lane, m = lanes(lv.nr), odd(lv.nr)

        def natural(i):
            g, j = slot_of(i, n)
            rows = pl.ds(lv.r0, lv.nr)
            low = pltpu.roll(zr[l][0][g, rows, :], (128 - n - 8 * j) % 128, axis=1)
            high = pltpu.roll(zr[l][1][g, rows, :], (n - 8 * j) % 128, axis=1)
            return jnp.where(lane < n, G[l][8 + i, rows, :], jnp.where(lane < 100, high, low))

        for p in range(lv.p0, lv.p0 + lv.np):
            a, b = natural(2 * (p - lv.po)), natural(2 * (p - lv.po) + 1)
            store_colours(l, p, a, b, m)

    def store_colours(l, p, a, b, m):
        lv = LEV[l]
        rows = pl.ds(lv.r0, lv.nr)
        red = jnp.where(m, b, a)
        FR[l][p, rows, :] = red
        FB[l][p, rows, :] = jnp.where(m, a, b)
        R[l][p, rows, :] = red * C[l][kind(l, p), 0]

    second = send_right_side(1)
    pack_first(lambda i: B[0][3 + i, 8:72, :], zs["v"], 32, 0, 61, 3)
    kept = exchange("v", ((B[0], H, 2, 3),), 3, 32, 8, 64, 3)
    wait_recv(second)
    split_right_side(1)
    black_sweep(1, True)
    restrict_to(1, G[2], 8, 16)
    third = send_right_side(2)
    wait_recv(third)
    split_right_side(2)
    black_sweep(2, True)

    lane8 = lanes(8)
    own3 = None
    for i in range(8):
        g = coarse_side(2, LEV[2].po + i)
        slot = lax.rem(gz + i, 16)
        g = pltpu.roll(jnp.where(lane8 < 8, g, 0.0), 8 * slot, axis=1)
        own3 = g if own3 is None else own3 + g
    pack3[...] = own3
    Z3[1, 1, gz] = own3

    def to_columns(act):
        for dx, dy in itertools.product((-1, 0, 1), repeat=2):

            def column(k, carry, dx=dx, dy=dy):
                @pl.when(k != gz)
                def _():
                    act(dx, dy, k)

                if (dx, dy) != (0, 0):

                    @pl.when(k == gz)
                    def _():
                        act(dx, dy, k)

                return carry

            yield dx, dy, column

    def start3(dx, dy, k):
        copy3(dx, dy, k).start()

    def copy3(dx, dy, k):
        at = (dx + 1) * 24 + (dy + 1) * 8
        return pltpu.make_async_remote_copy(
            pack3, Z3.at[1 - dx, 1 - dy, gz], sems["3"][0].at[at + k], sems["3"][1].at[at + gz], device_id=(gx + dx, gy + dy, k), device_id_type=MESH
        )

    def arrive3(dx, dy, k):
        at = (dx + 1) * 24 + (dy + 1) * 8
        pltpu.make_async_remote_copy(
            pack3, Z3.at[1 - dx, 1 - dy, k], sems["3"][0].at[at + k], sems["3"][1].at[at + k], device_id=(gx - dx, gy - dy, k), device_id_type=MESH
        ).wait_recv()

    def left3(dx, dy, k):
        copy3(dx, dy, k).wait_send()

    def over_columns(act, sign):
        for dx, dy, column in to_columns(act):

            @pl.when(inside((sign * dx, sign * dy, 0), me))
            def _(column=column):
                lax.fori_loop(0, SIDE, column, 0)

    over_columns(start3, 1)
    over_columns(arrive3, -1)

    m3 = odd(24)
    for p in range(1, 13):
        ab = []
        for i in (2 * (p - 1), 2 * (p - 1) + 1):
            x = i % 8
            tiles = []
            for cy in range(3):
                t = jnp.zeros((8, 128), F32)
                for k in range(SIDE):
                    s = 8 * ((x + k) % 16)
                    t = jnp.where((lane8 >= s) & (lane8 < s + 8), Z3[i // 8, cy, k], t)
                tiles.append(pltpu.roll(t, (128 - 8 * x) % 128, axis=1) if x else t)
            ab.append(jnp.concatenate(tiles, axis=0))
        store_colours(3, p, ab[0], ab[1], m3)
    black_sweep(3, True)

    lane4 = lanes(4)
    own4 = None
    for i in range(4):
        g = jnp.where(lane4 < 32, coarse_side(3, LEV[3].po + i), 0.0)
        g = pltpu.roll(g, 32 * i, axis=1) if i else g
        own4 = g if own4 is None else own4 + g
    pack4[0:4, :] = own4
    pack4[4:8, :] = own4
    G4[gx, gy, 0:4, :] = own4

    def copy4(k):
        return pltpu.make_async_remote_copy(
            pack4, G4.at[gx, gy], sems["4"][0].at[k], sems["4"][1].at[gx * SIDE + gy], device_id=(k // SIDE, k % SIDE, gz), device_id_type=MESH
        )

    def over_plane(act):
        def body(k, carry):
            @pl.when(k != gx * SIDE + gy)
            def _():
                act(k)

            return carry

        lax.fori_loop(0, SIDE * SIDE, body, 0)

    over_plane(lambda k: copy4(k).start())
    over_plane(
        lambda k: pltpu.make_async_remote_copy(
            pack4, G4.at[k // SIDE, k % SIDE], sems["4"][0].at[k], sems["4"][1].at[k], device_id=(k // SIDE, k % SIDE, gz), device_id_type=MESH
        ).wait_recv()
    )
    for x, y in itertools.product(range(SIDE), repeat=2):
        A4[x, pl.ds(4 * y, 4), :] = G4[x, y, 0:4, :]
    m4 = odd(32)
    for x in range(SIDE):
        a = A4[x]
        parts = [a] + [pltpu.roll(a, 128 - 32 * i, axis=1) for i in (1, 2, 3)]
        store_colours(4, 4 + 2 * x, parts[0], parts[1], m4)
        store_colours(4, 5 + 2 * x, parts[2], parts[3], m4)
    for l in (4, 5):
        black_sweep(l, True)
        restrict_to(l, N[l + 1], 0, 0)
        lv = LEV[l + 1]
        m = odd(lv.nr)
        for p in range(lv.p0, lv.p0 + lv.np):
            store_colours(l + 1, p, N[l + 1][2 * (p - 1)], N[l + 1][2 * (p - 1) + 1], m)
    black_sweep(6, False)
    for _ in range(COARSE_SWEEPS - 1):
        red_sweep(6)
        black_sweep(6, False)

    def expand(l):
        lf, lc = LEV[l], LEV[l + 1]
        c0, cn, r0, rn = GIVE[l]
        fine0 = lf.oy + 2 * (r0 - lc.oy)
        if l == 3:
            c0, r0 = 2 * gx + 1, 4 * gy + 4
            fine0 = 8
        m = odd(rn)
        lane = lanes(rn)
        z = (jnp.where(lane < 100, lane, lane - 128) >> 1) + (8 * gz if l == 2 else 0)
        at, beside = z & 127, (z + 2 * (lane & 1) - 1) & 127

        def body(i):
            rows = pl.ds(r0, rn)
            r, b = R[l + 1][c0 + i, rows, :], B[l + 1][c0 + i, rows, :]
            for a, e in ((0, jnp.where(m, b, r)), (1, jnp.where(m, r, b))):
                here = jnp.take_along_axis(e, at, axis=1, mode="promise_in_bounds")
                there = jnp.take_along_axis(e, beside, axis=1, mode="promise_in_bounds")
                for k in (0, 1):
                    EX[l][2 * i + a, pl.ds(fine0 + k, rn, stride=2), :] = here
                    EZ[l][2 * i + a, pl.ds(fine0 + k, rn, stride=2), :] = there

        sweep_loop(0, cn, 4 if l == 0 else 16, body)

    def correct(l):
        lv = LEV[l]
        m = odd(lv.nr)
        second_row = (iota((lv.nr, 128), 0) & 1) == 1
        rows = pl.ds(lv.r0, lv.nr)

        def body(p):
            e = p - EDGE[l]
            t = kind(l, p)
            sides = jnp.where(m, EX[l][e - 1, rows, :], EX[l][e + 1, rows, :])
            sides = sides + jnp.where(second_row, EX[l][e, pl.ds(lv.r0 + 1, lv.nr), :], EX[l][e, pl.ds(lv.r0 - 1, lv.nr), :])
            add = EX[l][e, rows, :] * A[l][t] + (EZ[l][e, rows, :] + sides) * Q[l][t]
            return add, B[l]

        if l > 0:

            def plain(p):
                add, ref = body(p)
                ref[p, rows, :] = ref[p, rows, :] + add

            sweep_loop(lv.p0, lv.np, 12, plain)
        else:
            for i in range(-2, 34):
                g, j = slot_of(i, 32)
                p = 3 + i
                low, high = zr["v"][0][g, 4:76, :], zr["v"][1][g, 4:76, :]
                w = jnp.where(((lane72 - 8 * j) & 127) < 3, high, low)
                w = pltpu.roll(w, (64 - 8 * j) % 128, axis=1)
                add, ref = body(p)
                ref[p, rows, :] = jnp.where(lane72 < 64, H[p, rows, :], w) + add

    for l in (5, 4, 3, 2, 1, 0):
        expand(l)
        if l == 0:
            wait_recv(kept)
            wait_send(kept)
        correct(l)
        red_sweep(l)
        black_sweep(l, l == 0)

    lv = LEV[0]
    m = ((iota((64, 64), 0) + iota((64, 64), 1)) & 1) == 1

    def results(p):
        r, b = R[0][p, 8:72, 0:64], B[0][p, 8:72, 0:64]
        x = 2 * (p - lv.po)
        u_in[x] = jnp.where(m, b, r)
        u_in[x + 1] = jnp.where(m, r, b)
        r, b = red_residual(0, p)[:, 0:64], T[p, 8:72, 0:64]
        f_in[x] = jnp.where(m, b, r)
        f_in[x + 1] = jnp.where(m, r, b)

    copies_out = []
    for part in range(2):
        sweep_loop(3 + 16 * part, 16, 8, results)
        for i, (src, dst) in enumerate(((u_in, out_u), (f_in, out_r))):
            cut = pl.ds(32 * part, 32)
            copy = pltpu.make_async_copy(src.at[cut], dst.at[cut], out_sem.at[2 * part + i])
            copy.start()
            copies_out.append(copy)
    wait_send(second)
    wait_send(third)
    over_columns(left3, 1)
    over_plane(lambda k: copy4(k).wait_send())
    for copy in copies_out:
        copy.wait()


EDGE = {0: -1, 1: -1, 2: -1, 3: -1, 4: 2, 5: -1}


def inside(d, me):
    ok = None
    for step, at in zip(d, me):
        if step:
            here = (at > 0) if step < 0 else (at < SIDE - 1)
            ok = here if ok is None else ok & here
    return True if ok is None else ok


def vmem(*shape):
    return pltpu.VMEM(shape, F32)


def per_device(right_side, guess):
    whole = vmem(64, 64, 64)
    scratch = [whole, whole]
    for _ in range(4):
        scratch += [vmem(*lv.shape()) for lv in LEV]
    for _ in range(2):
        scratch += [vmem(4, 2, lv.nr, 128) for lv in LEV]
    for _ in range(2):
        scratch += [vmem(4, lv.nr, 128) for lv in LEV[:6]]
    for _ in range(2):
        scratch += [vmem(2 * GIVE[l][1], LEV[l].rows, 128) for l in range(6)]
    scratch += [vmem(*LEV[0].shape())] * 2
    scratch += [vmem(48, 64, 128), vmem(32, 48, 128)]
    scratch += [vmem(16, 16, 128), vmem(8, 8, 128)]
    packed = ((2, 64, 80), (2, 64, 80), (2, 32, 64), (1, 16, 48))
    for groups, n, _ in packed:
        scratch += [vmem(groups, n, 128)] * 2
    for groups, _, rows in packed:
        scratch += [vmem(groups + 2, rows, 128)] * 2
    scratch += [vmem(8, 128), vmem(3, 3, 8, 8, 128), vmem(8, 128), vmem(8, 8, 8, 128), vmem(8, 32, 128)]
    for copies in (42, 26, 26, 26, 72, 64):
        scratch += [pltpu.SemaphoreType.DMA((copies,))] * 2
    scratch += [pltpu.SemaphoreType.DMA((2,)), pltpu.SemaphoreType.DMA((4,))]
    block = jax.ShapeDtypeStruct(right_side.shape, F32)
    return pl.pallas_call(
        kernel,
        out_shape=(block, block),
        in_specs=[pl.BlockSpec(memory_space=pl.ANY)] * 2,
        out_specs=(pl.BlockSpec(memory_space=pl.ANY),) * 2,
        scratch_shapes=scratch,
        compiler_params=pltpu.CompilerParams(collective_id=0, has_side_effects=True, vmem_limit_bytes=60 * 2**20),
    )(right_side, guess)


def solution(mesh):
    spec = P("gx", "gy", "gz")
    return jax.shard_map(per_device, mesh=mesh, in_specs=(spec, spec), out_specs=(spec, spec), check_vma=False)
```

time: 1430 us -> 82.4 us (0.06); the launches traced: 1410 us -> 82.3 us
  starting transfers between devices: 523 us -> 0 us
  local copies, waits for them, and re-layouts: 304 us -> 4.63 us
  waiting for transfers between devices: 248 us -> 0 us
  other arithmetic: 226 us -> 0 us
  blocking collectives: 94.9 us -> 0 us
  Pallas kernels: 0 us -> 77 us
    ppermute x186 -> x0, starting transfers between devices: 523 us -> none  [the longest x93 367 us: padded_2(): before = lax.ppermute(last, axis, up)]
    ppermute x186 -> x0, waiting for transfers between devices: 248 us -> none  [the longest x93 231 us: padded_2(): after = lax.ppermute(leading, axis, down)]
    unnamed x1 -> x0, blocking collectives: 94.9 us -> none
    select_n x52 -> x0, other arithmetic: 89.2 us -> none  [the longest x26 81 us: relax(): return jnp.where(colour, updated, padded[1:-1, 1:-1, 1:-1])]
    reshape x5 -> x0, local copies, waits for them, and re-layouts: 81.6 us -> none  [restrict(): remainder.reshape(shape[0] // 2, 2, shape[1] // 2, 2, shape[2] // 2, 2)]
    pallas_call x0 -> x1, Pallas kernels: none -> 77 us  [per_device(): pl.pallas_call(kernel, out_shape=(block, block), in_specs=[pl.BlockSpec(m...]
    slice x91 -> x0, local copies, waits for them, and re-layouts: 72.9 us -> none  [the longest x38 49.4 us: padded_2(): leading = lax.slice_in_dim(value, 0, width, axis=dim)]
    add x5 -> x0, local copies, waits for them, and re-layouts: 65.3 us -> none  [prolong(): centre[:, None, :, None, :, None] + along_first + along_second + along_third]
  transfers between devices with their start and end apart: 186 -> 0, of which waited for: 96 -> 0; matrix products, arithmetic and copies ran while one was open for 3% -> 0% of each run, Pallas kernels for 0% -> 0%
where the time goes in v1:
time: 82.4 us; the launch traced here: 82.3 us
  Pallas kernels  77 us (93%)
  local copies, waits for them, and re-layouts  4.63 us (6%)
    pallas_call x1, Pallas kernels, per_device(): pl.pallas_call(kernel, out_shape=(block, block), in_specs=[pl.BlockSpec(m...  77 us
    unnamed x4, local copies, waits for them, and re-layouts  4.63 us

profile of v1, /device:TPU:1, one launch (start us, length us, event | category | flops | bytes accessed | tf_op | source)
XLA Modules:
  0.0 82.3 jit_solution(9487835955125259816)
XLA Ops:
  0.6 77.0 %shard_map.41 = (f32[64,64,64]{2,1,0:T(8,128)}, f32[64,64,64]{2,1,0:T(8,128)}) custom-call(f32[64,64,64]{2,1,0:T(8,128)} %refs_0_.1, f32[64,64,64]{2,1,0:T(8,128)} %refs_1_.1), custom_call_target="tpu_custom_call" | custom-call | tf_op jit(solution)/shard_map/pallas_call | solution.py:707
  77.7 0.0 copy-start
  77.7 3.3 %copy.6 = f32[64,64,64]{2,1,0:T(8,128)} copy(f32[64,64,64]{2,1,0:T(8,128)} %get-tuple-element.4) | data formatting | bytes 2097152
  81.0 0.0 copy-done
  81.0 1.3 %copy.7 = f32[64,64,64]{2,1,0:T(8,128)} copy(f32[64,64,64]{2,1,0:T(8,128)S(1)} %copy-done) | data formatting | bytes 2097152
Async XLA Ops:
  77.7 3.3 %copy-start = (f32[64,64,64]{2,1,0:T(8,128)S(1)}, f32[64,64,64]{2,1,0:T(8,128)}, u32[]{:S(2)}) copy-start(f32[64,64,64]{2,1,0:T(8,128)} %get-tuple-element.5) | copy-start | bytes 3145732

commit v2 on v1

v2 whole, which is shorter than its diff:
```python
import itertools

import jax
import jax.numpy as jnp
from jax import lax
from jax.experimental import pallas as pl
from jax.experimental.pallas import tpu as pltpu
from jax.sharding import PartitionSpec as P

COARSE_SWEEPS = 4
MESH = pl.DeviceIdType.MESH
SIDE = 8
F32 = jnp.float32


class Level:
    def __init__(self, n, total, po, oy, p0, np_, r0, nr, pairs, rows, whole_z):
        self.n, self.total, self.po, self.oy = n, total, po, oy
        self.p0, self.np, self.r0, self.nr = p0, np_, r0, nr
        self.pairs, self.rows, self.whole_z = pairs, rows, whole_z

    def shape(self):
        return (self.pairs, self.rows, 128)


LEV = [
    Level(64, 512, 3, 8, 1, 36, 4, 72, 38, 80, False),
    Level(32, 256, 5, 16, 1, 24, 8, 48, 26, 64, False),
    Level(16, 128, 5, 16, 1, 16, 8, 32, 18, 48, False),
    Level(8, 64, 5, 16, 1, 12, 8, 24, 14, 40, True),
    Level(32, 32, 4, 8, 4, 16, 8, 32, 24, 48, True),
    Level(16, 16, 1, 8, 1, 8, 8, 16, 10, 32, True),
    Level(8, 8, 1, 8, 1, 4, 8, 8, 6, 24, True),
]
GIVE = {0: (3, 20, 12, 40), 1: (2, 14, 12, 24), 2: (2, 10, 12, 16), 3: (0, 8, 0, 12), 4: (0, 10, 8, 16), 5: (0, 6, 8, 8)}
PHASES = ("f", "v", 1, 2, "3", "4")
WIDTH = {1: 6, 2: 7}


def iota(shape, axis):
    return lax.broadcasted_iota(jnp.int32, shape, axis)


def odd():
    return ((iota((8, 128), 0) + iota((8, 128), 1)) & 1) == 1


def lanes():
    return iota((8, 128), 1)


def pick(mask, a, b):
    shape = a.shape
    if shape[0] <= 8:
        return jnp.where(mask[: shape[0]], a, b)
    tiles = (shape[0] // 8, 8, 128)
    return jnp.where(mask[None], a.reshape(tiles), b.reshape(tiles)).reshape(shape)


def within(start, width):
    return ((lanes() - start) & 127) < width


def turn(a, shift):
    return pltpu.roll(a, shift % 128, axis=1) if shift % 128 else a


def take(a, index):
    return jnp.take_along_axis(a, index, axis=1, mode="promise_in_bounds")


def lane_index(rows):
    return iota((rows, 128), 1)


def sweep_loop(start, count, step, body):
    step = max(k for k in range(1, step + 1) if count % k == 0)
    if count == step:
        for i in range(count):
            body(start + i)
        return

    def some(j, carry):
        for i in range(step):
            body(start + j * step + i)
        return carry

    lax.fori_loop(0, count // step, some, 0)


def around(src, p, r0, nr, up):
    here = src[p, pl.ds(r0, nr), :]
    side = pick(up, src[p + 1, pl.ds(r0, nr), :], src[p - 1, pl.ds(r0, nr), :])
    rows = src[p, pl.ds(r0 - 1, nr), :] + src[p, pl.ds(r0 + 1, nr), :]
    return (here + side) + rows + (pltpu.roll(here, 1, axis=1) + pltpu.roll(here, 127, axis=1))


def kernel(*refs):
    it = iter(refs)
    f_hbm, u_hbm, u_out, r_out = (next(it) for _ in range(4))
    f_in, u_in = next(it), next(it)
    R = [next(it) for _ in range(7)]
    B = [next(it) for _ in range(7)]
    FR = [next(it) for _ in range(7)]
    FB = [next(it) for _ in range(7)]
    C = [next(it) for _ in range(7)]
    D = [next(it) for _ in range(7)]
    A = [next(it) for _ in range(6)]
    Q = [next(it) for _ in range(6)]
    EX = [next(it) for _ in range(6)]
    EZ = [next(it) for _ in range(6)]
    T, H = next(it), next(it)
    G = {1: next(it), 2: next(it)}
    PS = {1: next(it), 2: next(it)}
    PR = {1: next(it), 2: next(it)}
    N = {5: next(it), 6: next(it)}
    zs = {k: (next(it), next(it)) for k in ("f", "v", 1, 2)}
    zr = {k: (next(it), next(it)) for k in ("f", "v", 1, 2)}
    pack3, Z3, pack4, G4, tally = (next(it) for _ in range(5))
    send_sem, recv_sem, in_sem, token = (next(it) for _ in range(4))

    gx, gy, gz = lax.axis_index("gx"), lax.axis_index("gy"), lax.axis_index("gz")
    me = (gx, gy, gz)

    copies_in = []
    for i, (src, dst) in enumerate(((u_hbm, u_in), (f_hbm, f_in))):
        copy = pltpu.make_async_copy(src, dst, in_sem.at[i])
        copy.start()
        copies_in.append(copy)

    barrier = pltpu.get_barrier_semaphore()
    rooms = [jnp.where((at > 0) & (at < SIDE - 1), 3, 2) for at in me]
    for d in itertools.product((-1, 0, 1), repeat=3):
        if d != (0, 0, 0):

            @pl.when(inside(d, me))
            def _(d=d):
                pl.semaphore_signal(barrier, inc=1, device_id=tuple(at + step for at, step in zip(me, d)), device_id_type=MESH)

    pl.semaphore_wait(barrier, rooms[0] * rooms[1] * rooms[2] - 1)

    def tokens(k, far, act):
        count = jnp.int32(0)
        for d in itertools.product((-1, 0, 1), repeat=3):
            if d == (0, 0, 0) or (d[2] and (d[0] or d[1])):
                continue
            there = inside(d, me, far)
            count = count + jnp.where(there, 1, 0)
            if act:

                @pl.when(there)
                def _(d=d):
                    device = tuple(at + far * step for at, step in zip(me, d))
                    pl.semaphore_signal(token.at[k], inc=1, device_id=device, device_id_type=MESH)

        if not act:
            pl.semaphore_wait(token.at[k], count)

    lv = LEV[0]
    m64 = ((iota((64, 64), 0) + iota((64, 64), 1)) & 1) == 1
    for copy in copies_in:
        copy.wait()

    def apart(p):
        a, b = u_in[2 * (p - lv.po)], u_in[2 * (p - lv.po) + 1]
        B[0][p, 8:72, 0:64] = jnp.where(m64, a, b)
        a, b = f_in[2 * (p - lv.po)], f_in[2 * (p - lv.po) + 1]
        FR[0][p, 8:72, 0:64] = jnp.where(m64, b, a)
        FB[0][p, 8:72, 0:64] = jnp.where(m64, a, b)

    sweep_loop(3, 32, 8, apart)

    def pack_faces(get, out, count, low, high, width, apart):
        for g in range(count // 16):
            lo = hi = None
            for j in range(16):
                t = get(16 * g + j)
                a = turn(t, 8 * j)
                b = turn(t, 8 * j + apart) if apart else a
                if lo is None:
                    lo, hi = a, b
                else:
                    lo = pick(within(low + 8 * j, width), a, lo)
                    hi = pick(within(high + apart + 8 * j, width), b, hi)
            out[0][g] = lo
            out[1][g] = hi

    at_fb = within(5, 1) | within(68, 1)
    at_fr = within(3, 2) | within(65, 2)

    def face_first(i):
        t = pick(at_fb, turn(FB[0][3 + i, 8:72, :], 5), B[0][3 + i, 8:72, :])
        return pick(at_fr, turn(FR[0][3 + i, 8:72, :], 3), t)

    pack_faces(face_first, zs["f"], 32, 0, 61, 8, 0)

    at_edge = [(at == 0) | (at == SIDE - 1) for at in me]

    def exchange(key, arrays, oy, n, hz):
        k = PHASES.index(key)
        groups = zs[key][0].shape[0]
        total = dict.fromkeys(itertools.product((False, True), repeat=3), 0)
        for d in sorted(itertools.product((-1, 0, 1), repeat=3), key=lambda d: -sum(map(abs, d))):
            if d == (0, 0, 0):
                continue
            dx, dy, dz = d
            pieces = []
            if dz == 0:
                for src, ps, dst, pd, own, hp, hr in arrays:
                    s0, d0, w = {-1: (ps, pd + own, hp), 0: (ps, pd, own), 1: (ps + own - hp, pd - hp, hp)}[dx]
                    rs, rd, rw = {-1: (0, oy + n, hr), 0: (0, oy, n), 1: (n - hr, oy - hr, hr)}[dy]
                    rs = rs + (oy if src.shape[1] > n else 0)
                    pieces.append((src.at[pl.ds(s0, w), pl.ds(rs, rw), :], dst.at[pl.ds(d0, w), pl.ds(rd, rw), :], w * rw))
            else:
                s0, d0, w = {-1: (0, groups + 1, 1), 0: (0, 1, groups), 1: (groups - 1, 0, 1)}[dx]
                rs, rd, rw = {-1: (0, oy + n, hz), 0: (0, oy, n), 1: (n - hz, oy - hz, hz)}[dy]
                src, dst = (zs[key][0], zr[key][1]) if dz < 0 else (zs[key][1], zr[key][0])
                pieces.append((src.at[pl.ds(s0, w), pl.ds(rs, rw), :], dst.at[pl.ds(d0, w), pl.ds(rd, rw), :], w * rw))

            @pl.when(inside(d, me))
            def _(d=d, pieces=pieces):
                device = tuple(at + step for at, step in zip(me, d))
                for src, dst, _ in pieces:
                    pltpu.make_async_remote_copy(
                        src, dst, send_sem.at[k], recv_sem.at[k], device_id=device, device_id_type=MESH
                    ).start()

            for edge in total:
                if not any(e and step > 0 for e, step in zip(edge, d)):
                    total[edge] += sum(rows for _, _, rows in pieces)
        return k, total

    def settle(what, arrived, left):
        k, total = what
        other = tuple(jnp.where(at == 0, at + 1, at - 1) for at in me)
        for edge, rows in total.items():
            same = None
            for e, here in zip(edge, at_edge):
                t = here if e else jnp.logical_not(here)
                same = t if same is None else same & t

            @pl.when(same)
            def _(rows=rows):
                cut = tally.at[pl.ds(0, rows), :]
                copy = pltpu.make_async_remote_copy(cut, cut, send_sem.at[k], recv_sem.at[k], device_id=other, device_id_type=MESH)
                if arrived:
                    copy.wait_recv()
                if left:
                    copy.wait_send()

    first = exchange("f", [(ref, 3, ref, 3, 32, hp, hr) for ref, hp, hr in ((B[0], 2, 3), (FR[0], 1, 2), (FB[0], 1, 1))], 8, 64, 3)

    def outside(ref, po, own, hp, oy, n, hr):
        planes, rows = ref.shape[0], ref.shape[1]
        for cond, cut in (
            (gx == 0, (slice(po - hp, po), slice(0, rows))),
            (gx == SIDE - 1, (slice(po + own, po + own + hp), slice(0, rows))),
            (gy == 0, (slice(0, planes), slice(oy - hr, oy))),
            (gy == SIDE - 1, (slice(0, planes), slice(oy + n, oy + n + hr))),
        ):

            @pl.when(cond)
            def _(cut=cut):
                shape = (cut[1].stop - cut[1].start, 128)
                for p in range(cut[0].start, cut[0].stop):
                    ref[p, cut[1], :] = jnp.zeros(shape, F32)

    def outside_z(key):
        for side, cond in ((0, gz == 0), (1, gz == SIDE - 1)):

            @pl.when(cond)
            def _(side=side):
                ref = zr[key][side]
                ref[...] = jnp.zeros(ref.shape, F32)

    def edges_z(key, po, n, hz, oy, groups):
        for side in (0, 1):
            ref = zr[key][side]
            rows = ref.shape[1]
            for cond, cut in (
                (gx == 0, (0, 1, 0, rows)),
                (gx == SIDE - 1, (groups + 1, 1, 0, rows)),
                (gy == 0, (0, groups + 2, oy - hz, hz)),
                (gy == SIDE - 1, (0, groups + 2, oy + n, hz)),
            ):

                @pl.when(cond)
                def _(cut=cut, ref=ref):
                    ref[pl.ds(cut[0], cut[1]), pl.ds(cut[2], cut[3]), :] = jnp.zeros((cut[1], cut[3], 128), F32)

    for ref, hp, hr in ((B[0], 2, 3), (FR[0], 1, 2), (FB[0], 1, 1), (H, 2, 3)):
        outside(ref, 3, 32, hp, 8, 64, hr)
    for key, n, oy, groups, hz in (("f", 64, 8, 2, 3), ("v", 64, 8, 2, 3), (1, 32, 16, 2, 6), (2, 16, 16, 1, 7)):
        outside_z(key)
        edges_z(key, 3, n, hz, oy, groups)
    outside(PR[1], 2, 8, 2, 16, 32, 8)
    outside(PR[2], 1, 2, 1, 16, 16, 8)
    for dx, dy in itertools.product((-1, 0, 1), repeat=2):
        if (dx, dy) != (0, 0):

            @pl.when(jnp.logical_not(inside((dx, dy, 0), me)))
            def _(dx=dx, dy=dy):
                Z3[dx + 1, dy + 1] = jnp.zeros((SIDE, 8, 128), F32)

    for l in (4, 5, 6):
        R[l][...] = jnp.zeros(LEV[l].shape(), F32)
        B[l][...] = jnp.zeros(LEV[l].shape(), F32)
    for l in (4, 5):
        EX[l][...] = jnp.zeros(EX[l].shape, F32)

    def tables(l):
        lv = LEV[l]
        shape = (lv.nr, 128)
        row, lane = iota(shape, 0) + lv.r0, iota(shape, 1)
        y = row - lv.oy
        z = jnp.where(lane < 100, lane, lane - 128)
        if l < 4:
            y = y + gy * lv.n
        if l < 3:
            z = z + gz * lv.n
        last = lv.total - 1
        within = (y >= 0) & (y <= last) & (z >= 0) & (z <= last)
        one = lambda c: jnp.where(c, 1, 0)
        w = one(y == 0) + one(y == last) + one(z == 0) + one(z == last)
        high = one(((row + lane) & 1) == 1)
        for kind, colour in itertools.product(range(3), range(2)):
            a = high if colour == 0 else 1 - high
            d = w if kind == 0 else (w + 1 - a if kind == 1 else w + a)
            inv = jnp.where(d == 0, 1 / 6, jnp.where(d == 1, 1 / 7, jnp.where(d == 2, 1 / 8, 1 / 9)))
            C[l][kind, colour] = jnp.where(within, inv, 0.0)
            D[l][kind, colour] = 6.0 + d.astype(F32)
            if colour == 1 and l < 6:
                q = jnp.where(within, 0.25, 0.0)
                Q[l][kind] = q
                A[l][kind] = (1.0 - d.astype(F32)) * q
        for colour in range(2):
            C[l][3, colour] = jnp.zeros(shape, F32)
            D[l][3, colour] = jnp.full(shape, 6.0, F32)
        if l < 6:
            Q[l][3] = jnp.zeros(shape, F32)
            A[l][3] = jnp.zeros(shape, F32)

    for l in range(7):
        tables(l)

    def kind(l, p):
        lv = LEV[l]
        x = 2 * (p - lv.po) + (gx * lv.n if l < 4 else 0)
        if l >= 4:
            return jnp.where(x == 0, 1, jnp.where(x == lv.total - 2, 2, 0))
        return jnp.where(x == 0, 1, jnp.where(x == lv.total - 2, 2, jnp.where((x < 0) | (x >= lv.total), 3, 0)))

    settle(first, True, True)
    tokens(0, 2, True)
    lane, m = lanes(), odd()
    not_m = jnp.logical_not(m)

    def slot_of(i, n):
        groups = n // 16
        if i < 0:
            return 0, 16 + i
        if i >= n:
            return groups + 1, i - n
        return 1 + i // 16, i % 16

    def unpack_first(i):
        g, j = slot_of(i, 32)
        low, high = zr["f"][0][g, 4:76, :], zr["f"][1][g, 4:76, :]
        for ref, at, width, shift in ((B[0], 0, 3, 64), (FR[0], 3, 2, 61), (FB[0], 5, 1, 59)):
            w = turn(pick(within(8 * j + at, width), high, low), shift - 8 * j)
            ref[3 + i, 4:76, :] = pick(lane < 64, ref[3 + i, 4:76, :], w)

    for i in range(-2, 34):
        unpack_first(i)

    def red_sweep(l):
        lv = LEV[l]

        def body(p):
            s = around(B[l], p, lv.r0, lv.nr, m)
            R[l][p, pl.ds(lv.r0, lv.nr), :] = (FR[l][p, pl.ds(lv.r0, lv.nr), :] + s) * C[l][kind(l, p), 0]

        sweep_loop(lv.p0, lv.np, 36, body)

    def black_sweep(l, keep):
        lv = LEV[l]

        def body(p):
            t = kind(l, p)
            rows = pl.ds(lv.r0, lv.nr)
            fs = FB[l][p, rows, :] + around(R[l], p, lv.r0, lv.nr, not_m)
            b = fs * C[l][t, 1]
            B[l][p, rows, :] = b
            if keep:
                T[p, rows, :] = fs - D[l][t, 1] * b

        sweep_loop(lv.p0, lv.np, 36, body)

    def red_residual(l, p):
        lv = LEV[l]
        s = around(B[l], p, lv.oy, lv.n, m)
        at = lv.oy - lv.r0
        return FR[l][p, pl.ds(lv.oy, lv.n), :] + s - D[l][kind(l, p), 0, pl.ds(at, lv.n), :] * R[l][p, pl.ds(lv.oy, lv.n), :]

    def residual(l):
        lv = LEV[l]

        def body(p):
            T[p, pl.ds(lv.oy, lv.n), :] = T[p, pl.ds(lv.oy, lv.n), :] + red_residual(l, p)

        sweep_loop(lv.po, lv.n // 2, 16, body)

    def coarse_side(l, p):
        lv = LEV[l]
        half = lv.n // 2
        u = T[p, pl.ds(lv.oy, half, stride=2), :] + T[p, pl.ds(lv.oy + 1, half, stride=2), :]
        z = 2 * lane_index(half)
        return 0.5 * (take(u, z & 127) + take(u, (z + 1) & 127))

    red_sweep(0)
    black_sweep(0, True)

    def keep_black(p):
        H[p, 8:72, :] = B[0][p, 8:72, :]

    sweep_loop(3, 32, 8, keep_black)

    def restrict_to(l, dst, first_plane, first_row):
        lv = LEV[l]

        def body(p):
            dst[p - lv.po + first_plane, pl.ds(first_row, lv.n // 2), :] = coarse_side(l, p)

        sweep_loop(lv.po, lv.n // 2, 16, body)

    residual(0)
    restrict_to(0, G[1], 0, 0)

    def send_right_side(l):
        n, w = LEV[l].n, WIDTH[l]
        per = 128 // n
        for q in range(n // per):
            t = G[l][per * q]
            for j in range(1, per):
                t = pick(within(n * j, n), turn(G[l][per * q + j], n * j), t)
            PS[l][q] = t
        pack_faces(lambda i: G[l][i], zs[l], n, 0, n - 8, 8, 128 - 2 * n)
        wide = 8 // per
        return exchange(l, [(PS[l], 0, PR[l], wide, n // per, wide, w)], 16, n, w)

    def split_right_side(l):
        lv = LEV[l]
        n = lv.n
        per = 128 // n

        def natural(i):
            g, j = slot_of(i, n)
            rows = pl.ds(lv.r0, lv.nr)
            side = pick(within(8 * j, 8), zr[l][1][g, rows, :], zr[l][0][g, rows, :])
            q, k = (i + 8) // per, (i + 8) % per
            if 0 <= i < n:
                below, above = (turn(PR[l][q, pl.ds(r, 8), :], -n * k) for r in (8, 16 + n))
                here = jnp.concatenate([below, G[l][i], above], axis=0)
            else:
                here = turn(PR[l][q, rows, :], -n * k)
            return pick(lane < n, here, turn(side, n - 8 * j))

        for p in range(lv.p0, lv.p0 + lv.np):
            a, b = natural(2 * (p - lv.po)), natural(2 * (p - lv.po) + 1)
            store_colours(l, p, a, b)

    def store_colours(l, p, a, b):
        lv = LEV[l]
        rows = pl.ds(lv.r0, lv.nr)
        red = pick(m, b, a)
        FR[l][p, rows, :] = red
        FB[l][p, rows, :] = pick(m, a, b)
        R[l][p, rows, :] = red * C[l][kind(l, p), 0]

    second = send_right_side(1)
    tokens(0, 2, False)
    tokens(1, 4, True)
    pack_faces(lambda i: B[0][3 + i, 8:72, :], zs["v"], 32, 0, 61, 3, 0)
    kept = exchange("v", [(B[0], 3, H, 3, 32, 2, 3)], 8, 64, 3)
    settle(second, True, False)
    split_right_side(1)
    black_sweep(1, True)
    residual(1)
    restrict_to(1, G[2], 0, 0)
    third = send_right_side(2)
    settle(third, True, False)
    split_right_side(2)
    black_sweep(2, True)
    residual(2)

    own3 = None
    for i in range(8):
        g = pick(lane < 8, coarse_side(2, LEV[2].po + i), jnp.zeros((8, 128), F32))
        g = pltpu.roll(g, 8 * lax.rem(gz + i, 16), axis=1)
        own3 = g if own3 is None else own3 + g
    pack3[...] = own3
    Z3[1, 1, gz] = own3
    tokens(1, 4, False)

    k3 = PHASES.index("3")
    for dx, dy in itertools.product((-1, 0, 1), repeat=2):

        def column(k, carry, dx=dx, dy=dy):
            @pl.when((k != gz) | ((dx, dy) != (0, 0)))
            def _():
                pltpu.make_async_remote_copy(
                    pack3, Z3.at[1 - dx, 1 - dy, gz], send_sem.at[k3], recv_sem.at[k3], device_id=(gx + dx, gy + dy, k), device_id_type=MESH
                ).start()

            return carry

        @pl.when(inside((dx, dy, 0), me))
        def _(column=column):
            lax.fori_loop(0, SIDE, column, 0)

    blocks = {edge: 8 * ((2 if edge[0] else 3) * (2 if edge[1] else 3) * SIDE - 1) for edge in itertools.product((False, True), repeat=3)}
    settle((k3, blocks), True, False)

    for p in range(1, 13):
        ab = []
        for i in (2 * (p - 1), 2 * (p - 1) + 1):
            x = i % 8
            tiles = []
            for cy in range(3):
                t = jnp.zeros((8, 128), F32)
                for k in range(SIDE):
                    t = jnp.where(within(8 * (x + k), 8), Z3[i // 8, cy, k], t)
                tiles.append(turn(t, -8 * x))
            ab.append(jnp.concatenate(tiles, axis=0))
        store_colours(3, p, ab[0], ab[1])
    black_sweep(3, True)

    residual(3)
    own4 = None
    for i in range(4):
        g = turn(pick(lane < 32, coarse_side(3, LEV[3].po + i), jnp.zeros((4, 128), F32)), 32 * i)
        own4 = g if own4 is None else own4 + g
    pack4[0:4, :] = own4
    G4[gx, pl.ds(4 * gy, 4), :] = own4

    k4 = PHASES.index("4")

    def column4(k, carry):
        x, y = k // SIDE, k % SIDE

        @pl.when((x != gx) | (y != gy))
        def _():
            pltpu.make_async_remote_copy(
                pack4.at[pl.ds(0, 4), :],
                G4.at[gx, pl.ds(4 * gy, 4), :],
                send_sem.at[k4],
                recv_sem.at[k4],
                device_id=(x, y, gz),
                device_id_type=MESH,
            ).start()

        return carry

    lax.fori_loop(0, SIDE * SIDE, column4, 0)
    plane = (k4, dict.fromkeys(itertools.product((False, True), repeat=3), 4 * (SIDE * SIDE - 1)))
    settle(plane, True, False)
    for x in range(SIDE):
        parts = [turn(G4[x], -32 * i) for i in range(4)]
        store_colours(4, 4 + 2 * x, parts[0], parts[1])
        store_colours(4, 5 + 2 * x, parts[2], parts[3])
    for l in (4, 5):
        black_sweep(l, True)
        residual(l)
        restrict_to(l, N[l + 1], 0, 0)
        lv = LEV[l + 1]
        for p in range(lv.p0, lv.p0 + lv.np):
            store_colours(l + 1, p, N[l + 1][2 * (p - 1)], N[l + 1][2 * (p - 1) + 1])
    black_sweep(6, False)
    for _ in range(COARSE_SWEEPS - 1):
        red_sweep(6)
        black_sweep(6, False)

    def expand(l):
        lf, lc = LEV[l], LEV[l + 1]
        c0, cn, r0, rn = GIVE[l]
        fine0 = lf.oy + 2 * (r0 - lc.oy)
        if l == 3:
            c0, r0 = 2 * gx + 1, 4 * gy + 4
            fine0 = 8
        zf = lane_index(rn)
        z = (jnp.where(zf < 100, zf, zf - 128) >> 1) + (8 * gz if l == 2 else 0)
        at, beside = z & 127, (z + 2 * (zf & 1) - 1) & 127

        def body(i):
            rows = pl.ds(r0, rn)
            r, b = R[l + 1][c0 + i, rows, :], B[l + 1][c0 + i, rows, :]
            if rn % 8:
                mm = ((iota((rn, 128), 0) + iota((rn, 128), 1)) & 1) == 1
                both = jnp.where(mm, b, r), jnp.where(mm, r, b)
            else:
                both = pick(m, b, r), pick(m, r, b)
            for a, e in enumerate(both):
                here, there = take(e, at), take(e, beside)
                for k in (0, 1):
                    EX[l][2 * i + a, pl.ds(fine0 + k, rn, stride=2), :] = here
                    EZ[l][2 * i + a, pl.ds(fine0 + k, rn, stride=2), :] = there

        sweep_loop(0, cn, 20, body)

    def correct(l):
        lv = LEV[l]
        second_row = (iota((8, 128), 0) & 1) == 1
        rows = pl.ds(lv.r0, lv.nr)

        def body(p):
            e = p - EDGE[l]
            t = kind(l, p)
            sides = pick(m, EX[l][e - 1, rows, :], EX[l][e + 1, rows, :])
            sides = sides + pick(second_row, EX[l][e, pl.ds(lv.r0 + 1, lv.nr), :], EX[l][e, pl.ds(lv.r0 - 1, lv.nr), :])
            add = EX[l][e, rows, :] * A[l][t] + (EZ[l][e, rows, :] + sides) * Q[l][t]
            return add, B[l]

        if l > 0:

            def plain(p):
                add, ref = body(p)
                ref[p, rows, :] = ref[p, rows, :] + add

            sweep_loop(lv.p0, lv.np, 12, plain)
        else:
            for i in range(-2, 34):
                g, j = slot_of(i, 32)
                p = 3 + i
                low, high = zr["v"][0][g, 4:76, :], zr["v"][1][g, 4:76, :]
                w = turn(pick(within(8 * j, 3), high, low), 64 - 8 * j)
                add, ref = body(p)
                ref[p, rows, :] = pick(lane < 64, H[p, rows, :], w) + add

    for l in (5, 4):
        expand(l)
        correct(l)
        red_sweep(l)
        black_sweep(l, False)
    expand(3)
    correct(3)
    red_sweep(3)
    black_sweep(3, False)
    expand(2)
    correct(2)
    red_sweep(2)
    black_sweep(2, False)
    expand(1)
    correct(1)
    red_sweep(1)
    black_sweep(1, False)
    expand(0)
    settle(kept, True, True)
    correct(0)
    red_sweep(0)
    black_sweep(0, True)

    lv = LEV[0]

    def results(p):
        r, b = R[0][p, 8:72, :], B[0][p, 8:72, :]
        x = 2 * (p - lv.po)
        u_out[x] = pick(m, b, r)[:, 0:64]
        u_out[x + 1] = pick(m, r, b)[:, 0:64]
        r, b = red_residual(0, p), T[p, 8:72, :]
        r_out[x] = pick(m, b, r)[:, 0:64]
        r_out[x + 1] = pick(m, r, b)[:, 0:64]

    sweep_loop(3, 32, 32, results)
    for what in (second, third, (k3, blocks), plane):
        settle(what, False, True)


EDGE = {0: -1, 1: -1, 2: -1, 3: -1, 4: 2, 5: -1}


def inside(d, me, far=1):
    ok = None
    for step, at in zip(d, me):
        if step:
            here = (at >= far) if step < 0 else (at < SIDE - far)
            ok = here if ok is None else ok & here
    return True if ok is None else ok


def vmem(*shape):
    return pltpu.VMEM(shape, F32)


def per_device(right_side, guess):
    whole = vmem(64, 64, 64)
    scratch = [whole, whole]
    for _ in range(4):
        scratch += [vmem(*lv.shape()) for lv in LEV]
    for _ in range(2):
        scratch += [vmem(4, 2, lv.nr, 128) for lv in LEV]
    for _ in range(2):
        scratch += [vmem(4, lv.nr, 128) for lv in LEV[:6]]
    for _ in range(2):
        scratch += [vmem(2 * GIVE[l][1], LEV[l].rows, 128) for l in range(6)]
    scratch += [vmem(*LEV[0].shape())] * 2
    scratch += [vmem(32, 32, 128), vmem(16, 16, 128)]
    scratch += [vmem(8, 32, 128), vmem(2, 16, 128), vmem(12, 64, 128), vmem(4, 48, 128)]
    scratch += [vmem(16, 16, 128), vmem(8, 8, 128)]
    packed = ((2, 64, 80), (2, 64, 80), (2, 32, 64), (1, 16, 48))
    for groups, n, _ in packed:
        scratch += [vmem(groups, n, 128)] * 2
    for groups, _, rows in packed:
        scratch += [vmem(groups + 2, rows, 128)] * 2
    scratch += [vmem(8, 128), vmem(3, 3, 8, 8, 128), vmem(8, 128), vmem(8, 32, 128), vmem(2048, 128)]
    dma = pltpu.SemaphoreType.DMA((len(PHASES),))
    scratch += [dma, dma, pltpu.SemaphoreType.DMA((2,)), pltpu.SemaphoreType.REGULAR((2,))]
    block = pltpu.VMEM(right_side.shape, F32)
    return pl.pallas_call(
        kernel,
        out_shape=(block, block),
        in_specs=[pl.BlockSpec(memory_space=pl.ANY)] * 2,
        out_specs=(pl.BlockSpec(memory_space=pltpu.VMEM),) * 2,
        scratch_shapes=scratch,
        compiler_params=pltpu.CompilerParams(collective_id=0, has_side_effects=True, vmem_limit_bytes=50 * 2**20),
    )(right_side, guess)


def solution(mesh):
    spec = P("gx", "gy", "gz")
    return jax.shard_map(per_device, mesh=mesh, in_specs=(spec, spec), out_specs=(spec, spec), check_vma=False)
```

time: 82.4 us -> 64.6 us (0.78)
  Pallas kernels: 77 us -> 61.2 us
  local copies, waits for them, and re-layouts: 4.63 us -> 2.64 us
    pallas_call x1, Pallas kernels: 77 us -> 61.2 us  [per_device(): pl.pallas_call(kernel, out_shape=(block, block), in_specs=[pl.BlockSpec(m...]
    unnamed x4 -> x2, local copies, waits for them, and re-layouts: 4.63 us -> 2.64 us
where the time goes in v2:
time: 64.6 us; the launch traced here: 64.5 us
  Pallas kernels  61.2 us (95%)
  local copies, waits for them, and re-layouts  2.64 us (4%)
    pallas_call x1, Pallas kernels, per_device(): pl.pallas_call(kernel, out_shape=(block, block), in_specs=[pl.BlockSpec(m...  61.2 us
    unnamed x2, local copies, waits for them, and re-layouts  2.64 us

profile of v2, /device:TPU:1, one launch (start us, length us, event | category | flops | bytes accessed | tf_op | source)
XLA Modules:
  0.0 64.5 jit_solution(9693481616156350210)
XLA Ops:
  0.6 61.2 %shard_map.41 = (f32[64,64,64]{2,1,0:T(8,128)S(1)}, f32[64,64,64]{2,1,0:T(8,128)S(1)}) custom-call(f32[64,64,64]{2,1,0:T(8,128)} %refs_0_.1, f32[64,64,64]{2,1,0:T(8,128)} %refs_1_.1), custom_call_target="tpu_custom_call" | custom-call | tf_op jit(solution)/shard_map/pallas_call | solution.py:718
  61.8 1.3 %copy.6 = f32[64,64,64]{2,1,0:T(8,128)} copy(f32[64,64,64]{2,1,0:T(8,128)S(1)} %get-tuple-element.2) | data formatting | bytes 2097152
  63.2 1.3 %copy.7 = f32[64,64,64]{2,1,0:T(8,128)} copy(f32[64,64,64]{2,1,0:T(8,128)S(1)} %get-tuple-element.3) | data formatting | bytes 2097152

commit v3 on v2

--- a/solution.py
+++ b/solution.py
@@ -97,19 +97,21 @@
 
 def kernel(*refs):
     it = iter(refs)
-    f_hbm, u_hbm, u_out, r_out = (next(it) for _ in range(4))
+    f_hbm, u_hbm, R0, B0, FR0, T, D0 = (next(it) for _ in range(7))
     f_in, u_in = next(it), next(it)
-    R = [next(it) for _ in range(7)]
-    B = [next(it) for _ in range(7)]
-    FR = [next(it) for _ in range(7)]
+    R = [R0] + [next(it) for _ in range(6)]
+    B = [B0] + [next(it) for _ in range(6)]
+    FR = [FR0] + [next(it) for _ in range(6)]
     FB = [next(it) for _ in range(7)]
     C = [next(it) for _ in range(7)]
-    D = [next(it) for _ in range(7)]
+    D = [D0] + [next(it) for _ in range(6)]
     A = [next(it) for _ in range(6)]
     Q = [next(it) for _ in range(6)]
     EX = [next(it) for _ in range(6)]
     EZ = [next(it) for _ in range(6)]
-    T, H = next(it), next(it)
+    H = next(it)
+    xs, xr = (next(it), next(it)), (next(it), next(it))
+    ys, yr = (next(it), next(it)), (next(it), next(it))
     G = {1: next(it), 2: next(it)}
     PS = {1: next(it), 2: next(it)}
     PR = {1: next(it), 2: next(it)}
@@ -185,50 +187,56 @@
             out[0][g] = lo
             out[1][g] = hi
 
-    at_fb = within(5, 1) | within(68, 1)
-    at_fr = within(3, 2) | within(65, 2)
-
-    def face_first(i):
-        t = pick(at_fb, turn(FB[0][3 + i, 8:72, :], 5), B[0][3 + i, 8:72, :])
-        return pick(at_fr, turn(FR[0][3 + i, 8:72, :], 3), t)
-
-    pack_faces(face_first, zs["f"], 32, 0, 61, 8, 0)
-
     at_edge = [(at == 0) | (at == SIDE - 1) for at in me]
 
-    def exchange(key, arrays, oy, n, hz):
+    def halo(key, directions, pieces):
         k = PHASES.index(key)
-        groups = zs[key][0].shape[0]
-        total = dict.fromkeys(itertools.product((False, True), repeat=3), 0)
-        for d in sorted(itertools.product((-1, 0, 1), repeat=3), key=lambda d: -sum(map(abs, d))):
-            if d == (0, 0, 0):
-                continue
-            dx, dy, dz = d
-            pieces = []
-            if dz == 0:
-                for src, ps, dst, pd, own, hp, hr in arrays:
-                    s0, d0, w = {-1: (ps, pd + own, hp), 0: (ps, pd, own), 1: (ps + own - hp, pd - hp, hp)}[dx]
-                    rs, rd, rw = {-1: (0, oy + n, hr), 0: (0, oy, n), 1: (n - hr, oy - hr, hr)}[dy]
-                    rs = rs + (oy if src.shape[1] > n else 0)
-                    pieces.append((src.at[pl.ds(s0, w), pl.ds(rs, rw), :], dst.at[pl.ds(d0, w), pl.ds(rd, rw), :], w * rw))
-            else:
-                s0, d0, w = {-1: (0, groups + 1, 1), 0: (0, 1, groups), 1: (groups - 1, 0, 1)}[dx]
-                rs, rd, rw = {-1: (0, oy + n, hz), 0: (0, oy, n), 1: (n - hz, oy - hz, hz)}[dy]
-                src, dst = (zs[key][0], zr[key][1]) if dz < 0 else (zs[key][1], zr[key][0])
-                pieces.append((src.at[pl.ds(s0, w), pl.ds(rs, rw), :], dst.at[pl.ds(d0, w), pl.ds(rd, rw), :], w * rw))
+        total = dict.fromkeys(EDGES, 0)
+        for d in directions:
+            copies = pieces(d)
 
             @pl.when(inside(d, me))
-            def _(d=d, pieces=pieces):
+            def _(d=d, copies=copies):
                 device = tuple(at + step for at, step in zip(me, d))
-                for src, dst, _ in pieces:
+                for src, dst, _ in copies:
                     pltpu.make_async_remote_copy(
                         src, dst, send_sem.at[k], recv_sem.at[k], device_id=device, device_id_type=MESH
                     ).start()
 
             for edge in total:
                 if not any(e and step > 0 for e, step in zip(edge, d)):
-                    total[edge] += sum(rows for _, _, rows in pieces)
+                    total[edge] += sum(rows for _, _, rows in copies)
         return k, total
+
+    def both(a, b):
+        return a[0], {edge: a[1][edge] + b[1][edge] for edge in EDGES}
+
+    def sides(arrays, oy, n):
+        def pieces(d):
+            out = []
+            for src, ps, dst, pd, own, hp, hr in arrays:
+                s0, d0, w = {-1: (ps, pd + own, hp), 0: (ps, pd, own), 1: (ps + own - hp, pd - hp, hp)}[d[0]]
+                rs, rd, rw = {-1: (0, oy + n, hr), 0: (0, oy, n), 1: (n - hr, oy - hr, hr)}[d[1]]
+                rs = rs + (oy if src.shape[1] > n else 0)
+                out.append((src.at[pl.ds(s0, w), pl.ds(rs, rw), :], dst.at[pl.ds(d0, w), pl.ds(rd, rw), :], w * rw))
+            return out
+
+        return pieces
+
+    def faces(key, oy, n, hz):
+        groups = zs[key][0].shape[0]
+
+        def pieces(d):
+            s0, d0, w = {-1: (0, groups + 1, 1), 0: (0, 1, groups), 1: (groups - 1, 0, 1)}[d[0]]
+            rs, rd, rw = {-1: (0, oy + n, hz), 0: (0, oy, n), 1: (n - hz, oy - hz, hz)}[d[1]]
+            src, dst = (zs[key][0], zr[key][1]) if d[2] < 0 else (zs[key][1], zr[key][0])
+            return [(src.at[pl.ds(s0, w), pl.ds(rs, rw), :], dst.at[pl.ds(d0, w), pl.ds(rd, rw), :], w * rw)]
+
+        return pieces
+
+    def exchange(key, arrays, oy, n, hz):
+        packed = halo(key, ACROSS, faces(key, oy, n, hz))
+        return both(packed, halo(key, FLAT, sides(arrays, oy, n)))
 
     def settle(what, arrived, left):
         k, total = what
@@ -248,7 +256,38 @@
                 if left:
                     copy.wait_send()
 
-    first = exchange("f", [(ref, 3, ref, 3, 32, hp, hr) for ref, hp, hr in ((B[0], 2, 3), (FR[0], 1, 2), (FB[0], 1, 1))], 8, 64, 3)
+    lane, m = lanes(), odd()
+    not_m = jnp.logical_not(m)
+    for side, (near, next_) in enumerate(((3, 4), (34, 33))):
+        for k, (a, other) in enumerate(((near, FR[0]), (next_, FB[0]))):
+            xs[side][k] = pick(lane < 64, B[0][a, 8:72, :], turn(other[near, 8:72, :], 64))
+
+    def first_sides(d):
+        side = 0 if d[0] < 0 else 1
+        rs, rd, rw = {-1: (0, 72, 3), 0: (0, 8, 64), 1: (61, 5, 3)}[d[1]]
+        return [(xs[side].at[:, pl.ds(rs, rw), :], xr[1 - side].at[:, pl.ds(rd, rw), :], 2 * rw)]
+
+    first = halo("f", [d for d in FLAT if d[0]], first_sides)
+    third_row = iota((8, 128), 0) == 2
+    for i in range(32):
+        p = 3 + i
+        for side, (rb, rr, rk) in enumerate(((8, 8, 6), (69, 70, 69))):
+            t = turn(jnp.where(third_row, FB[0][p, rk : rk + 8, :], FR[0][p, rr : rr + 8, :]), 64)
+            ys[side][i] = jnp.where(lane < 64, B[0][p, rb : rb + 8, :], t)
+
+    def first_rows(d):
+        side = 0 if d[1] < 0 else 1
+        return [(ys[side].at[:, pl.ds(0, 3), :], yr[1 - side].at[:, pl.ds(0, 3), :], 96)]
+
+    first = both(first, halo("f", [d for d in FLAT if not d[0]], first_rows))
+    at_fb = within(5, 1) | within(68, 1)
+    at_fr = within(3, 2) | within(65, 2)
+
+    for p in range(3, 35):
+        t = pick(at_fb, turn(FB[0][p, 8:72, :], 5), B[0][p, 8:72, :])
+        T[p, 8:72, :] = pick(at_fr, turn(FR[0][p, 8:72, :], 3), t)
+    pack_faces(lambda i: T[3 + i, 8:72, :], zs["f"], 32, 0, 61, 8, 0)
+    first = both(first, halo("f", ACROSS, faces("f", 8, 64, 3)))
 
     def outside(ref, po, own, hp, oy, n, hr):
         planes, rows = ref.shape[0], ref.shape[1]
@@ -288,8 +327,21 @@
                 def _(cut=cut, ref=ref):
                     ref[pl.ds(cut[0], cut[1]), pl.ds(cut[2], cut[3]), :] = jnp.zeros((cut[1], cut[3], 128), F32)
 
-    for ref, hp, hr in ((B[0], 2, 3), (FR[0], 1, 2), (FB[0], 1, 1), (H, 2, 3)):
-        outside(ref, 3, 32, hp, 8, 64, hr)
+    outside(H, 3, 32, 2, 8, 64, 3)
+    for i in range(2):
+        for cond, refs0 in ((gx == (0, SIDE - 1)[i], (xr[i],)), (gy == (0, SIDE - 1)[i], (yr[i],))):
+
+            @pl.when(cond)
+            def _(refs0=refs0):
+                for ref in refs0:
+                    ref[...] = jnp.zeros(ref.shape, F32)
+
+        @pl.when(gy == (0, SIDE - 1)[i])
+        def _(i=i):
+            for ref in xr:
+                for k in range(2):
+                    ref[k, pl.ds((5, 72)[i], 3), :] = jnp.zeros((3, 128), F32)
+
     for key, n, oy, groups, hz in (("f", 64, 8, 2, 3), ("v", 64, 8, 2, 3), (1, 32, 16, 2, 6), (2, 16, 16, 1, 7)):
         outside_z(key)
         edges_z(key, 3, n, hz, oy, groups)
@@ -300,7 +352,7 @@
 
             @pl.when(jnp.logical_not(inside((dx, dy, 0), me)))
             def _(dx=dx, dy=dy):
-                Z3[dx + 1, dy + 1] = jnp.zeros((SIDE, 8, 128), F32)
+                Z3[dx + 1, dy + 1] = jnp.zeros((4 * SIDE, 128), F32)
 
     for l in (4, 5, 6):
         R[l][...] = jnp.zeros(LEV[l].shape(), F32)
@@ -352,8 +404,6 @@
 
     settle(first, True, True)
     tokens(0, 2, True)
-    lane, m = lanes(), odd()
-    not_m = jnp.logical_not(m)
 
     def slot_of(i, n):
         groups = n // 16
@@ -370,6 +420,20 @@
             w = turn(pick(within(8 * j + at, width), high, low), shift - 8 * j)
             ref[3 + i, 4:76, :] = pick(lane < 64, ref[3 + i, 4:76, :], w)
 
+    for side, (near, next_) in enumerate(((2, 1), (35, 36))):
+        rows = pl.ds(4, 72)
+        a, b = xr[side][0, rows, :], xr[side][1, rows, :]
+        B[0][near, rows, :] = a
+        B[0][next_, rows, :] = b
+        FR[0][near, rows, :] = turn(a, 64)
+        FB[0][near, rows, :] = turn(b, 64)
+    for i in range(32):
+        for side, (rb, rr, rk) in enumerate(((5, 6, 7), (72, 72, 72))):
+            t = yr[side][i]
+            f = turn(t, 64)
+            B[0][3 + i, rb : rb + 3, :] = t[0:3]
+            FR[0][3 + i, rr : rr + 2, :] = f[0:2]
+            FB[0][3 + i, rk : rk + 1, :] = f[2:3]
     for i in range(-2, 34):
         unpack_first(i)
 
@@ -488,6 +552,11 @@
     residual(1)
     restrict_to(1, G[2], 0, 0)
     third = send_right_side(2)
+    settle(kept, True, True)
+    for i in range(-2, 34):
+        g, j = slot_of(i, 32)
+        w = turn(pick(within(8 * j, 3), zr["v"][1][g, 4:76, :], zr["v"][0][g, 4:76, :]), 64 - 8 * j)
+        H[3 + i, 4:76, :] = pick(lane < 64, H[3 + i, 4:76, :], w)
     settle(third, True, False)
     split_right_side(2)
     black_sweep(2, True)
@@ -495,30 +564,32 @@
 
     own3 = None
     for i in range(8):
-        g = pick(lane < 8, coarse_side(2, LEV[2].po + i), jnp.zeros((8, 128), F32))
-        g = pltpu.roll(g, 8 * lax.rem(gz + i, 16), axis=1)
+        g = jnp.where(lane < 8, coarse_side(2, LEV[2].po + i), 0.0)
+        g = pltpu.roll(g, 8 * lax.rem(gz + i, 8), axis=1)
         own3 = g if own3 is None else own3 + g
-    pack3[...] = own3
-    Z3[1, 1, gz] = own3
+    pack3[0:8, :] = own3
+    own3 = jnp.where(lane[0:4] < 64, pack3[0:4, :], turn(pack3[4:8, :], 64))
+    pack3[8:12, :] = own3
+    Z3[1, 1, pl.ds(4 * gz, 4), :] = own3
     tokens(1, 4, False)
 
     k3 = PHASES.index("3")
-    for dx, dy in itertools.product((-1, 0, 1), repeat=2):
-
-        def column(k, carry, dx=dx, dy=dy):
-            @pl.when((k != gz) | ((dx, dy) != (0, 0)))
-            def _():
-                pltpu.make_async_remote_copy(
-                    pack3, Z3.at[1 - dx, 1 - dy, gz], send_sem.at[k3], recv_sem.at[k3], device_id=(gx + dx, gy + dy, k), device_id_type=MESH
-                ).start()
-
-            return carry
+    for dx, dy in sorted(itertools.product((-1, 0, 1), repeat=2), key=lambda d: -abs(d[0]) - abs(d[1])):
 
         @pl.when(inside((dx, dy, 0), me))
-        def _(column=column):
-            lax.fori_loop(0, SIDE, column, 0)
-
-    blocks = {edge: 8 * ((2 if edge[0] else 3) * (2 if edge[1] else 3) * SIDE - 1) for edge in itertools.product((False, True), repeat=3)}
+        def _(dx=dx, dy=dy):
+            for far in (4, 3, 5, 2, 6, 1, 7, 0):
+                if (dx, dy, far) != (0, 0, 0):
+                    pltpu.make_async_remote_copy(
+                        pack3.at[pl.ds(8, 4), :],
+                        Z3.at[1 - dx, 1 - dy, pl.ds(4 * gz, 4), :],
+                        send_sem.at[k3],
+                        recv_sem.at[k3],
+                        device_id=(gx + dx, gy + dy, (gz + far) & (SIDE - 1)),
+                        device_id_type=MESH,
+                    ).start()
+
+    blocks = {edge: 4 * ((2 if edge[0] else 3) * (2 if edge[1] else 3) * SIDE - 1) for edge in EDGES}
     settle((k3, blocks), True, False)
 
     for p in range(1, 13):
@@ -527,9 +598,14 @@
             x = i % 8
             tiles = []
             for cy in range(3):
-                t = jnp.zeros((8, 128), F32)
+                t = None
                 for k in range(SIDE):
-                    t = jnp.where(within(8 * (x + k), 8), Z3[i // 8, cy, k], t)
+                    block = Z3[i // 8, cy, 4 * k : 4 * k + 4, :]
+                    s = 8 * ((x + k) % 8)
+                    t = block if t is None else jnp.where((within(s, 8) | within(s + 64, 8))[0:4], block, t)
+                other = turn(t, 64)
+                low = lane[0:4] < 64
+                t = jnp.concatenate([jnp.where(low, t, other), jnp.where(low, other, t)], axis=0)
                 tiles.append(turn(t, -8 * x))
             ab.append(jnp.concatenate(tiles, axis=0))
         store_colours(3, p, ab[0], ab[1])
@@ -545,24 +621,18 @@
 
     k4 = PHASES.index("4")
 
-    def column4(k, carry):
-        x, y = k // SIDE, k % SIDE
-
-        @pl.when((x != gx) | (y != gy))
-        def _():
+    ring = lambda k: min(k, SIDE - k)
+    for dx, dy in sorted(itertools.product(range(SIDE), repeat=2), key=lambda d: -ring(d[0]) - ring(d[1])):
+        if (dx, dy) != (0, 0):
             pltpu.make_async_remote_copy(
                 pack4.at[pl.ds(0, 4), :],
                 G4.at[gx, pl.ds(4 * gy, 4), :],
                 send_sem.at[k4],
                 recv_sem.at[k4],
-                device_id=(x, y, gz),
+                device_id=((gx + dx) & (SIDE - 1), (gy + dy) & (SIDE - 1), gz),
                 device_id_type=MESH,
             ).start()
-
-        return carry
-
-    lax.fori_loop(0, SIDE * SIDE, column4, 0)
-    plane = (k4, dict.fromkeys(itertools.product((False, True), repeat=3), 4 * (SIDE * SIDE - 1)))
+    plane = (k4, dict.fromkeys(EDGES, 4 * (SIDE * SIDE - 1)))
     settle(plane, True, False)
     for x in range(SIDE):
         parts = [turn(G4[x], -32 * i) for i in range(4)]
@@ -618,23 +688,14 @@
             sides = pick(m, EX[l][e - 1, rows, :], EX[l][e + 1, rows, :])
             sides = sides + pick(second_row, EX[l][e, pl.ds(lv.r0 + 1, lv.nr), :], EX[l][e, pl.ds(lv.r0 - 1, lv.nr), :])
             add = EX[l][e, rows, :] * A[l][t] + (EZ[l][e, rows, :] + sides) * Q[l][t]
-            return add, B[l]
-
-        if l > 0:
-
-            def plain(p):
-                add, ref = body(p)
-                ref[p, rows, :] = ref[p, rows, :] + add
-
-            sweep_loop(lv.p0, lv.np, 12, plain)
-        else:
-            for i in range(-2, 34):
-                g, j = slot_of(i, 32)
-                p = 3 + i
-                low, high = zr["v"][0][g, 4:76, :], zr["v"][1][g, 4:76, :]
-                w = turn(pick(within(8 * j, 3), high, low), 64 - 8 * j)
-                add, ref = body(p)
-                ref[p, rows, :] = pick(lane < 64, H[p, rows, :], w) + add
+            return add
+
+        start = B[l] if l else H
+
+        def plain(p):
+            B[l][p, rows, :] = start[p, rows, :] + body(p)
+
+        sweep_loop(lv.p0, lv.np, 36, plain)
 
     for l in (5, 4):
         expand(l)
@@ -654,27 +715,35 @@
     red_sweep(1)
     black_sweep(1, False)
     expand(0)
-    settle(kept, True, True)
     correct(0)
     red_sweep(0)
     black_sweep(0, True)
 
-    lv = LEV[0]
-
-    def results(p):
-        r, b = R[0][p, 8:72, :], B[0][p, 8:72, :]
-        x = 2 * (p - lv.po)
-        u_out[x] = pick(m, b, r)[:, 0:64]
-        u_out[x + 1] = pick(m, r, b)[:, 0:64]
-        r, b = red_residual(0, p), T[p, 8:72, :]
-        r_out[x] = pick(m, b, r)[:, 0:64]
-        r_out[x + 1] = pick(m, r, b)[:, 0:64]
-
-    sweep_loop(3, 32, 32, results)
     for what in (second, third, (k3, blocks), plane):
         settle(what, False, True)
 
 
+def results(R, B, FR, T, D, u_out, r_out):
+    lv = LEV[0]
+    m = odd()
+    first = lv.po + 8 * pl.program_id(0)
+    for k in range(8):
+        p = first + k
+        x = lax.axis_index("gx") * lv.n + 2 * (p - lv.po)
+        kind = jnp.where(x == 0, 1, jnp.where(x == lv.total - 2, 2, 0))
+        r, b = R[p, 8:72, :], B[p, 8:72, :]
+        u_out[2 * k] = pick(m, b, r)[:, 0:64]
+        u_out[2 * k + 1] = pick(m, r, b)[:, 0:64]
+        left = FR[p, 8:72, :] + around(B, p, lv.oy, lv.n, m) - D[kind, 0, 4:68, :] * r
+        b = T[p, 8:72, :]
+        r_out[2 * k] = pick(m, b, left)[:, 0:64]
+        r_out[2 * k + 1] = pick(m, left, b)[:, 0:64]
+
+
+EDGES = tuple(itertools.product((False, True), repeat=3))
+AROUND = sorted((d for d in itertools.product((-1, 0, 1), repeat=3) if any(d)), key=lambda d: -sum(map(abs, d)))
+FLAT = [d for d in AROUND if d[2] == 0]
+ACROSS = [d for d in AROUND if d[2]]
 EDGE = {0: -1, 1: -1, 2: -1, 3: -1, 4: 2, 5: -1}
 
 
@@ -694,15 +763,17 @@
 def per_device(right_side, guess):
     whole = vmem(64, 64, 64)
     scratch = [whole, whole]
-    for _ in range(4):
-        scratch += [vmem(*lv.shape()) for lv in LEV]
-    for _ in range(2):
-        scratch += [vmem(4, 2, lv.nr, 128) for lv in LEV]
+    for _ in range(3):
+        scratch += [vmem(*lv.shape()) for lv in LEV[1:]]
+    scratch += [vmem(*lv.shape()) for lv in LEV]
+    scratch += [vmem(4, 2, lv.nr, 128) for lv in LEV]
+    scratch += [vmem(4, 2, lv.nr, 128) for lv in LEV[1:]]
     for _ in range(2):
         scratch += [vmem(4, lv.nr, 128) for lv in LEV[:6]]
     for _ in range(2):
         scratch += [vmem(2 * GIVE[l][1], LEV[l].rows, 128) for l in range(6)]
-    scratch += [vmem(*LEV[0].shape())] * 2
+    scratch += [vmem(*LEV[0].shape())]
+    scratch += [vmem(2, 64, 128)] * 2 + [vmem(2, 80, 128)] * 2 + [vmem(32, 8, 128)] * 4
     scratch += [vmem(32, 32, 128), vmem(16, 16, 128)]
     scratch += [vmem(8, 32, 128), vmem(2, 16, 128), vmem(12, 64, 128), vmem(4, 48, 128)]
     scratch += [vmem(16, 16, 128), vmem(8, 8, 128)]
@@ -711,18 +782,27 @@
         scratch += [vmem(groups, n, 128)] * 2
     for groups, _, rows in packed:
         scratch += [vmem(groups + 2, rows, 128)] * 2
-    scratch += [vmem(8, 128), vmem(3, 3, 8, 8, 128), vmem(8, 128), vmem(8, 32, 128), vmem(2048, 128)]
+    scratch += [vmem(16, 128), vmem(3, 3, 32, 128), vmem(8, 128), vmem(8, 32, 128), vmem(2048, 128)]
     dma = pltpu.SemaphoreType.DMA((len(PHASES),))
     scratch += [dma, dma, pltpu.SemaphoreType.DMA((2,)), pltpu.SemaphoreType.REGULAR((2,))]
-    block = pltpu.VMEM(right_side.shape, F32)
+    level0 = pltpu.VMEM(LEV[0].shape(), F32)
+    parts = pl.pallas_call(
+        kernel,
+        out_shape=(level0,) * 4 + (pltpu.VMEM((4, 2, LEV[0].nr, 128), F32),),
+        in_specs=[pl.BlockSpec(memory_space=pl.ANY)] * 2,
+        out_specs=(pl.BlockSpec(memory_space=pltpu.VMEM),) * 5,
+        scratch_shapes=scratch,
+        compiler_params=pltpu.CompilerParams(collective_id=0, has_side_effects=True, vmem_limit_bytes=48 * 2**20),
+    )(right_side, guess)
+    block = jax.ShapeDtypeStruct(right_side.shape, F32)
     return pl.pallas_call(
-        kernel,
+        results,
+        grid=(4,),
         out_shape=(block, block),
-        in_specs=[pl.BlockSpec(memory_space=pl.ANY)] * 2,
-        out_specs=(pl.BlockSpec(memory_space=pltpu.VMEM),) * 2,
-        scratch_shapes=scratch,
-        compiler_params=pltpu.CompilerParams(collective_id=0, has_side_effects=True, vmem_limit_bytes=50 * 2**20),
-    )(right_side, guess)
+        in_specs=[pl.BlockSpec(memory_space=pltpu.VMEM)] * 5,
+        out_specs=(pl.BlockSpec((16, 64, 64), lambda i: (i, 0, 0)),) * 2,
+        compiler_params=pltpu.CompilerParams(vmem_limit_bytes=12 * 2**20),
+    )(*parts)
 
 
 def solution(mesh):

time: 64.6 us -> 58.8 us (0.910)
  Pallas kernels: 61.2 us -> 58 us
  local copies, waits for them, and re-layouts: 2.64 us -> 0 us
    pallas_call x1 -> x2, Pallas kernels: 61.2 us -> 58 us  [the longest x1 55.4 us: per_device(): pl.pallas_call(kernel, out_shape=(level0,) * 4 + (pltpu.VMEM((4, 2, LEV[0...]
    unnamed x2 -> x0, local copies, waits for them, and re-layouts: 2.64 us -> none
where the time goes in v3:
time: 58.8 us; the launch traced here: 58.6 us
  Pallas kernels  58 us (99%)
  between operations  0.64 us (1%)
    pallas_call x1, Pallas kernels, per_device(): pl.pallas_call(kernel, out_shape=(level0,) * 4 + (pltpu.VMEM((4, 2, LEV[0...  55.4 us
    pallas_call x1, Pallas kernels, per_device(): pl.pallas_call(results, grid=(4,), out_shape=(block, block), in_specs=[pl...  2.6 us

profile of v3, /device:TPU:1, one launch (start us, length us, event | category | flops | bytes accessed | tf_op | source)
XLA Modules:
  0.0 58.6 jit_solution(2740240579941679662)
XLA Ops:
  0.6 55.4 %shard_map.41 = (f32[38,80,128]{2,1,0:T(8,128)S(1)}, f32[38,80,128]{2,1,0:T(8,128)S(1)}, f32[38,80,128]{2,1,0:T(8,128)S(1)}, f32[38,80,128]{2,1,0:T(8,128)S(1)}, f32[4,2,72,128]{3,2,1,0:T(8,128)S(1)}) custom-call(f32[64,64,64]{2,1,0:T(8,128)} %refs_0_.1, f32[64,64,64]{2,1,0:T(8,128)} %refs_1_.1), custom_call_target="tpu_custom_call" | custom-call | tf_op jit(solution)/shard_map/pallas_call | solution.py:789
  56.0 2.6 %shard_map.42 = (f32[64,64,64]{2,1,0:T(8,128)}, f32[64,64,64]{2,1,0:T(8,128)}) custom-call(f32[38,80,128]{2,1,0:T(8,128)S(1)} %get-tuple-element.7.R, f32[38,80,128]{2,1,0:T(8,128)S(1)} %get-tuple-element.8.B, f32[38,80,128]{2,1,0:T(8,128)S(1)} %get-tuple-element.9.FR, f32[38,80,128]{2,1,0:T(8,128)S(1)} %get-tuple-element.10.T, ...), custom_call_target="tpu_custom_call" | custom-call | tf_op jit(solution)/shard_map/pallas_call | solution.py:798

commit v4 on v3

--- a/solution.py
+++ b/solution.py
@@ -33,6 +33,11 @@
     Level(8, 8, 1, 8, 1, 4, 8, 8, 6, 24, True),
 ]
 GIVE = {0: (3, 20, 12, 40), 1: (2, 14, 12, 24), 2: (2, 10, 12, 16), 3: (0, 8, 0, 12), 4: (0, 10, 8, 16), 5: (0, 6, 8, 8)}
+ALL = {4: (4, 16, 8, 32), 5: (1, 8, 8, 16), 6: (1, 4, 8, 8)}
+RED = {0: (2, 34, 4, 72), 1: (3, 20, 12, 40), 2: (2, 14, 8, 32), 3: (2, 10, 8, 24), **ALL}
+BLACK_DOWN = {0: (2, 34, 4, 72), 1: (2, 22, 8, 48), 2: (2, 14, 8, 32), 3: (2, 10, 8, 24), **ALL}
+BLACK_UP = {1: (3, 20, 12, 40), 2: (3, 12, 12, 24), 3: (3, 8, 12, 16), **ALL}
+CORRECTED = {0: (1, 36, 4, 72), 1: (2, 22, 8, 48), 2: (2, 14, 8, 32), 3: (2, 10, 8, 24), **ALL}
 PHASES = ("f", "v", 1, 2, "3", "4")
 WIDTH = {1: 6, 2: 7}
 
@@ -97,19 +102,19 @@
 
 def kernel(*refs):
     it = iter(refs)
-    f_hbm, u_hbm, R0, B0, FR0, T, D0 = (next(it) for _ in range(7))
+    f_hbm, u_hbm, R0, FR0, FB0, C0, D0 = (next(it) for _ in range(7))
     f_in, u_in = next(it), next(it)
     R = [R0] + [next(it) for _ in range(6)]
-    B = [B0] + [next(it) for _ in range(6)]
+    B = [next(it) for _ in range(7)]
     FR = [FR0] + [next(it) for _ in range(6)]
-    FB = [next(it) for _ in range(7)]
-    C = [next(it) for _ in range(7)]
+    FB = [FB0] + [next(it) for _ in range(6)]
+    C = [C0] + [next(it) for _ in range(6)]
     D = [D0] + [next(it) for _ in range(6)]
     A = [next(it) for _ in range(6)]
     Q = [next(it) for _ in range(6)]
     EX = [next(it) for _ in range(6)]
     EZ = [next(it) for _ in range(6)]
-    H = next(it)
+    T, H = next(it), next(it)
     xs, xr = (next(it), next(it)), (next(it), next(it))
     ys, yr = (next(it), next(it)), (next(it), next(it))
     G = {1: next(it), 2: next(it)}
@@ -124,11 +129,16 @@
     gx, gy, gz = lax.axis_index("gx"), lax.axis_index("gy"), lax.axis_index("gz")
     me = (gx, gy, gz)
 
-    copies_in = []
-    for i, (src, dst) in enumerate(((u_hbm, u_in), (f_hbm, f_in))):
-        copy = pltpu.make_async_copy(src, dst, in_sem.at[i])
-        copy.start()
-        copies_in.append(copy)
+    def fetch(c):
+        cut = pl.ds(32 * c, 32)
+        return [
+            pltpu.make_async_copy(src.at[cut], dst.at[cut], in_sem.at[2 * c + i])
+            for i, (src, dst) in enumerate(((u_hbm, u_in), (f_hbm, f_in)))
+        ]
+
+    for c in range(2):
+        for copy in fetch(c):
+            copy.start()
 
     barrier = pltpu.get_barrier_semaphore()
     rooms = [jnp.where((at > 0) & (at < SIDE - 1), 3, 2) for at in me]
@@ -138,8 +148,6 @@
             @pl.when(inside(d, me))
             def _(d=d):
                 pl.semaphore_signal(barrier, inc=1, device_id=tuple(at + step for at, step in zip(me, d)), device_id_type=MESH)
-
-    pl.semaphore_wait(barrier, rooms[0] * rooms[1] * rooms[2] - 1)
 
     def tokens(k, far, act):
         count = jnp.int32(0)
@@ -160,8 +168,11 @@
 
     lv = LEV[0]
     m64 = ((iota((64, 64), 0) + iota((64, 64), 1)) & 1) == 1
-    for copy in copies_in:
-        copy.wait()
+    lane, m = lanes(), odd()
+    not_m = jnp.logical_not(m)
+    at_fb = within(5, 1) | within(68, 1)
+    at_fr = within(3, 2) | within(65, 2)
+    third_row = iota((8, 128), 0) == 2
 
     def apart(p):
         a, b = u_in[2 * (p - lv.po)], u_in[2 * (p - lv.po) + 1]
@@ -170,13 +181,20 @@
         FR[0][p, 8:72, 0:64] = jnp.where(m64, b, a)
         FB[0][p, 8:72, 0:64] = jnp.where(m64, a, b)
 
-    sweep_loop(3, 32, 8, apart)
-
-    def pack_faces(get, out, count, low, high, width, apart):
-        for g in range(count // 16):
+    def faces_of(p):
+        for side, (rb, rr, rk) in enumerate(((8, 8, 6), (69, 70, 69))):
+            t = turn(jnp.where(third_row, FB[0][p, rk : rk + 8, :], FR[0][p, rr : rr + 8, :]), 64)
+            ys[side][p - 3] = jnp.where(lane < 64, B[0][p, rb : rb + 8, :], t)
+        t = pick(at_fb, turn(FB[0][p, 8:72, :], 5), B[0][p, 8:72, :])
+        T[p, 8:72, :] = pick(at_fr, turn(FR[0][p, 8:72, :], 3), t)
+
+    def pack_faces(get, out, count, low, high, width, apart, start=0):
+        for i0 in range(start, start + count, 16):
+            half = i0 % 16
             lo = hi = None
-            for j in range(16):
-                t = get(16 * g + j)
+            for i in range(i0, min(i0 + 16 - half, start + count)):
+                j = i % 16
+                t = get(i)
                 a = turn(t, 8 * j)
                 b = turn(t, 8 * j + apart) if apart else a
                 if lo is None:
@@ -184,8 +202,24 @@
                 else:
                     lo = pick(within(low + 8 * j, width), a, lo)
                     hi = pick(within(high + apart + 8 * j, width), b, hi)
-            out[0][g] = lo
-            out[1][g] = hi
+            if half:
+                lo = pick(within(low + 64, 64), lo, out[0][i0 // 16])
+                hi = pick(within(high + apart + 64, 64), hi, out[1][i0 // 16])
+            out[0][i0 // 16] = lo
+            out[1][i0 // 16] = hi
+
+    for c in range(2):
+        for copy in fetch(c):
+            copy.wait()
+        for p in range(3 + 16 * c, 19 + 16 * c):
+            apart(p)
+        for p in range(3 + 16 * c, 19 + 16 * c):
+            faces_of(p)
+        pack_faces(lambda i: T[3 + i, 8:72, :], zs["f"], 16, 0, 61, 8, 0, 16 * c)
+    for side, (near, next_) in enumerate(((3, 4), (34, 33))):
+        for k, (a, other) in enumerate(((near, FR[0]), (next_, FB[0]))):
+            xs[side][k] = pick(lane < 64, B[0][a, 8:72, :], turn(other[near, 8:72, :], 64))
+    pl.semaphore_wait(barrier, rooms[0] * rooms[1] * rooms[2] - 1)
 
     at_edge = [(at == 0) | (at == SIDE - 1) for at in me]
 
@@ -256,39 +290,17 @@
                 if left:
                     copy.wait_send()
 
-    lane, m = lanes(), odd()
-    not_m = jnp.logical_not(m)
-    for side, (near, next_) in enumerate(((3, 4), (34, 33))):
-        for k, (a, other) in enumerate(((near, FR[0]), (next_, FB[0]))):
-            xs[side][k] = pick(lane < 64, B[0][a, 8:72, :], turn(other[near, 8:72, :], 64))
-
     def first_sides(d):
         side = 0 if d[0] < 0 else 1
         rs, rd, rw = {-1: (0, 72, 3), 0: (0, 8, 64), 1: (61, 5, 3)}[d[1]]
         return [(xs[side].at[:, pl.ds(rs, rw), :], xr[1 - side].at[:, pl.ds(rd, rw), :], 2 * rw)]
 
-    first = halo("f", [d for d in FLAT if d[0]], first_sides)
-    third_row = iota((8, 128), 0) == 2
-    for i in range(32):
-        p = 3 + i
-        for side, (rb, rr, rk) in enumerate(((8, 8, 6), (69, 70, 69))):
-            t = turn(jnp.where(third_row, FB[0][p, rk : rk + 8, :], FR[0][p, rr : rr + 8, :]), 64)
-            ys[side][i] = jnp.where(lane < 64, B[0][p, rb : rb + 8, :], t)
-
     def first_rows(d):
         side = 0 if d[1] < 0 else 1
         return [(ys[side].at[:, pl.ds(0, 3), :], yr[1 - side].at[:, pl.ds(0, 3), :], 96)]
 
-    first = both(first, halo("f", [d for d in FLAT if not d[0]], first_rows))
-    at_fb = within(5, 1) | within(68, 1)
-    at_fr = within(3, 2) | within(65, 2)
-
-    for p in range(3, 35):
-        t = pick(at_fb, turn(FB[0][p, 8:72, :], 5), B[0][p, 8:72, :])
-        T[p, 8:72, :] = pick(at_fr, turn(FR[0][p, 8:72, :], 3), t)
-    pack_faces(lambda i: T[3 + i, 8:72, :], zs["f"], 32, 0, 61, 8, 0)
-    first = both(first, halo("f", ACROSS, faces("f", 8, 64, 3)))
-
+    first = halo("f", ACROSS, faces("f", 8, 64, 3))
+    first = both(first, halo("f", FLAT, lambda d: first_sides(d) if d[0] else first_rows(d)))
     def outside(ref, po, own, hp, oy, n, hr):
         planes, rows = ref.shape[0], ref.shape[1]
         for cond, cut in (
@@ -439,26 +451,28 @@
 
     def red_sweep(l):
         lv = LEV[l]
+        p0, count, r0, nr = RED[l]
+        rows, table = pl.ds(r0, nr), pl.ds(r0 - lv.r0, nr)
 
         def body(p):
-            s = around(B[l], p, lv.r0, lv.nr, m)
-            R[l][p, pl.ds(lv.r0, lv.nr), :] = (FR[l][p, pl.ds(lv.r0, lv.nr), :] + s) * C[l][kind(l, p), 0]
-
-        sweep_loop(lv.p0, lv.np, 36, body)
-
-    def black_sweep(l, keep):
-        lv = LEV[l]
+            R[l][p, rows, :] = (FR[l][p, rows, :] + around(B[l], p, r0, nr, m)) * C[l][kind(l, p), 0, table, :]
+
+        sweep_loop(p0, count, 36, body)
+
+    def black_sweep(l, region, keep):
+        lv = LEV[l]
+        p0, count, r0, nr = region[l]
+        rows, table = pl.ds(r0, nr), pl.ds(r0 - lv.r0, nr)
 
         def body(p):
             t = kind(l, p)
-            rows = pl.ds(lv.r0, lv.nr)
-            fs = FB[l][p, rows, :] + around(R[l], p, lv.r0, lv.nr, not_m)
-            b = fs * C[l][t, 1]
+            fs = FB[l][p, rows, :] + around(R[l], p, r0, nr, not_m)
+            b = fs * C[l][t, 1, table, :]
             B[l][p, rows, :] = b
             if keep:
-                T[p, rows, :] = fs - D[l][t, 1] * b
-
-        sweep_loop(lv.p0, lv.np, 36, body)
+                T[p, rows, :] = fs - D[l][t, 1, table, :] * b
+
+        sweep_loop(p0, count, 36, body)
 
     def red_residual(l, p):
         lv = LEV[l]
@@ -472,7 +486,7 @@
         def body(p):
             T[p, pl.ds(lv.oy, lv.n), :] = T[p, pl.ds(lv.oy, lv.n), :] + red_residual(l, p)
 
-        sweep_loop(lv.po, lv.n // 2, 16, body)
+        sweep_loop(lv.po, lv.n // 2, 32, body)
 
     def coarse_side(l, p):
         lv = LEV[l]
@@ -482,12 +496,7 @@
         return 0.5 * (take(u, z & 127) + take(u, (z + 1) & 127))
 
     red_sweep(0)
-    black_sweep(0, True)
-
-    def keep_black(p):
-        H[p, 8:72, :] = B[0][p, 8:72, :]
-
-    sweep_loop(3, 32, 8, keep_black)
+    black_sweep(0, BLACK_DOWN, True)
 
     def restrict_to(l, dst, first_plane, first_row):
         lv = LEV[l]
@@ -495,7 +504,7 @@
         def body(p):
             dst[p - lv.po + first_plane, pl.ds(first_row, lv.n // 2), :] = coarse_side(l, p)
 
-        sweep_loop(lv.po, lv.n // 2, 16, body)
+        sweep_loop(lv.po, lv.n // 2, 32, body)
 
     residual(0)
     restrict_to(0, G[1], 0, 0)
@@ -542,24 +551,24 @@
         R[l][p, rows, :] = red * C[l][kind(l, p), 0]
 
     second = send_right_side(1)
+    def keep_black(p):
+        H[p, 8:72, :] = B[0][p, 8:72, :]
+
+    sweep_loop(3, 32, 8, keep_black)
+
     tokens(0, 2, False)
     tokens(1, 4, True)
-    pack_faces(lambda i: B[0][3 + i, 8:72, :], zs["v"], 32, 0, 61, 3, 0)
-    kept = exchange("v", [(B[0], 3, H, 3, 32, 2, 3)], 8, 64, 3)
     settle(second, True, False)
     split_right_side(1)
-    black_sweep(1, True)
+    black_sweep(1, BLACK_DOWN, True)
     residual(1)
     restrict_to(1, G[2], 0, 0)
     third = send_right_side(2)
-    settle(kept, True, True)
-    for i in range(-2, 34):
-        g, j = slot_of(i, 32)
-        w = turn(pick(within(8 * j, 3), zr["v"][1][g, 4:76, :], zr["v"][0][g, 4:76, :]), 64 - 8 * j)
-        H[3 + i, 4:76, :] = pick(lane < 64, H[3 + i, 4:76, :], w)
+    pack_faces(lambda i: B[0][3 + i, 8:72, :], zs["v"], 32, 0, 61, 3, 0)
+    kept = exchange("v", [(B[0], 3, H, 3, 32, 2, 3)], 8, 64, 3)
     settle(third, True, False)
     split_right_side(2)
-    black_sweep(2, True)
+    black_sweep(2, BLACK_DOWN, True)
     residual(2)
 
     own3 = None
@@ -609,7 +618,7 @@
                 tiles.append(turn(t, -8 * x))
             ab.append(jnp.concatenate(tiles, axis=0))
         store_colours(3, p, ab[0], ab[1])
-    black_sweep(3, True)
+    black_sweep(3, BLACK_DOWN, True)
 
     residual(3)
     own4 = None
@@ -633,22 +642,27 @@
                 device_id_type=MESH,
             ).start()
     plane = (k4, dict.fromkeys(EDGES, 4 * (SIDE * SIDE - 1)))
+    settle(kept, True, True)
+    for i in range(-2, 34):
+        g, j = slot_of(i, 32)
+        w = turn(pick(within(8 * j, 3), zr["v"][1][g, 4:76, :], zr["v"][0][g, 4:76, :]), 64 - 8 * j)
+        H[3 + i, 4:76, :] = pick(lane < 64, H[3 + i, 4:76, :], w)
     settle(plane, True, False)
     for x in range(SIDE):
         parts = [turn(G4[x], -32 * i) for i in range(4)]
         store_colours(4, 4 + 2 * x, parts[0], parts[1])
         store_colours(4, 5 + 2 * x, parts[2], parts[3])
     for l in (4, 5):
-        black_sweep(l, True)
+        black_sweep(l, BLACK_DOWN, True)
         residual(l)
         restrict_to(l, N[l + 1], 0, 0)
         lv = LEV[l + 1]
         for p in range(lv.p0, lv.p0 + lv.np):
             store_colours(l + 1, p, N[l + 1][2 * (p - 1)], N[l + 1][2 * (p - 1) + 1])
-    black_sweep(6, False)
+    black_sweep(6, BLACK_UP, False)
     for _ in range(COARSE_SWEEPS - 1):
         red_sweep(6)
-        black_sweep(6, False)
+        black_sweep(6, BLACK_UP, False)
 
     def expand(l):
         lf, lc = LEV[l], LEV[l + 1]
@@ -680,14 +694,15 @@
     def correct(l):
         lv = LEV[l]
         second_row = (iota((8, 128), 0) & 1) == 1
-        rows = pl.ds(lv.r0, lv.nr)
+        p0, count, r0, nr = CORRECTED[l]
+        rows, table = pl.ds(r0, nr), pl.ds(r0 - lv.r0, nr)
 
         def body(p):
             e = p - EDGE[l]
             t = kind(l, p)
             sides = pick(m, EX[l][e - 1, rows, :], EX[l][e + 1, rows, :])
-            sides = sides + pick(second_row, EX[l][e, pl.ds(lv.r0 + 1, lv.nr), :], EX[l][e, pl.ds(lv.r0 - 1, lv.nr), :])
-            add = EX[l][e, rows, :] * A[l][t] + (EZ[l][e, rows, :] + sides) * Q[l][t]
+            sides = sides + pick(second_row, EX[l][e, pl.ds(r0 + 1, nr), :], EX[l][e, pl.ds(r0 - 1, nr), :])
+            add = EX[l][e, rows, :] * A[l][t, table, :] + (EZ[l][e, rows, :] + sides) * Q[l][t, table, :]
             return add
 
         start = B[l] if l else H
@@ -695,51 +710,77 @@
         def plain(p):
             B[l][p, rows, :] = start[p, rows, :] + body(p)
 
-        sweep_loop(lv.p0, lv.np, 36, plain)
+        sweep_loop(p0, count, 36, plain)
 
     for l in (5, 4):
         expand(l)
         correct(l)
         red_sweep(l)
-        black_sweep(l, False)
+        black_sweep(l, BLACK_UP, False)
     expand(3)
     correct(3)
     red_sweep(3)
-    black_sweep(3, False)
+    black_sweep(3, BLACK_UP, False)
     expand(2)
     correct(2)
     red_sweep(2)
-    black_sweep(2, False)
+    black_sweep(2, BLACK_UP, False)
     expand(1)
     correct(1)
     red_sweep(1)
-    black_sweep(1, False)
+    black_sweep(1, BLACK_UP, False)
     expand(0)
     correct(0)
     red_sweep(0)
-    black_sweep(0, True)
-
     for what in (second, third, (k3, blocks), plane):
         settle(what, False, True)
 
 
-def results(R, B, FR, T, D, u_out, r_out):
+def results(R, FR, FB, C, D, u_hbm, r_hbm, B, T, u_out, r_out, sem):
     lv = LEV[0]
     m = odd()
-    first = lv.po + 8 * pl.program_id(0)
-    for k in range(8):
-        p = first + k
+    not_m = jnp.logical_not(m)
+
+    def kind(p):
         x = lax.axis_index("gx") * lv.n + 2 * (p - lv.po)
-        kind = jnp.where(x == 0, 1, jnp.where(x == lv.total - 2, 2, 0))
+        return jnp.where(x == 0, 1, jnp.where(x == lv.total - 2, 2, jnp.where((x < 0) | (x >= lv.total), 3, 0)))
+
+    def black(p):
+        t = kind(p)
+        fs = FB[p, 4:76, :] + around(R, p, 4, 72, not_m)
+        b = fs * C[t, 1]
+        B[p, 4:76, :] = b
+        T[p, 4:76, :] = fs - D[t, 1] * b
+
+    def finish(p):
+        x = 2 * (p - lv.po)
         r, b = R[p, 8:72, :], B[p, 8:72, :]
-        u_out[2 * k] = pick(m, b, r)[:, 0:64]
-        u_out[2 * k + 1] = pick(m, r, b)[:, 0:64]
-        left = FR[p, 8:72, :] + around(B, p, lv.oy, lv.n, m) - D[kind, 0, 4:68, :] * r
+        u_out[x] = pick(m, b, r)[:, 0:64]
+        u_out[x + 1] = pick(m, r, b)[:, 0:64]
+        left = FR[p, 8:72, :] + around(B, p, lv.oy, lv.n, m) - D[kind(p), 0, 4:68, :] * r
         b = T[p, 8:72, :]
-        r_out[2 * k] = pick(m, b, left)[:, 0:64]
-        r_out[2 * k + 1] = pick(m, left, b)[:, 0:64]
-
-
+        r_out[x] = pick(m, b, left)[:, 0:64]
+        r_out[x + 1] = pick(m, left, b)[:, 0:64]
+
+    done, first, copies = 2, 3, []
+    for part in PARTS:
+        ready = min(first + part + (PARTS[0] if first == 3 else part), 35)
+        for p in range(done, ready + 1):
+            black(p)
+        done = ready + 1
+        for p in range(first, first + part):
+            finish(p)
+        cut = pl.ds(2 * (first - 3), 2 * part)
+        for src, dst in ((u_out, u_hbm), (r_out, r_hbm)):
+            copy = pltpu.make_async_copy(src.at[cut], dst.at[cut], sem.at[len(copies)])
+            copy.start()
+            copies.append(copy)
+        first += part
+    for copy in copies:
+        copy.wait()
+
+
+PARTS = (4, 4, 4, 4, 4, 4, 4, 4)
 EDGES = tuple(itertools.product((False, True), repeat=3))
 AROUND = sorted((d for d in itertools.product((-1, 0, 1), repeat=3) if any(d)), key=lambda d: -sum(map(abs, d)))
 FLAT = [d for d in AROUND if d[2] == 0]
@@ -763,16 +804,17 @@
 def per_device(right_side, guess):
     whole = vmem(64, 64, 64)
     scratch = [whole, whole]
-    for _ in range(3):
+    scratch += [vmem(*lv.shape()) for lv in LEV[1:]]
+    scratch += [vmem(*lv.shape()) for lv in LEV]
+    for _ in range(2):
         scratch += [vmem(*lv.shape()) for lv in LEV[1:]]
-    scratch += [vmem(*lv.shape()) for lv in LEV]
-    scratch += [vmem(4, 2, lv.nr, 128) for lv in LEV]
-    scratch += [vmem(4, 2, lv.nr, 128) for lv in LEV[1:]]
+    for _ in range(2):
+        scratch += [vmem(4, 2, lv.nr, 128) for lv in LEV[1:]]
     for _ in range(2):
         scratch += [vmem(4, lv.nr, 128) for lv in LEV[:6]]
     for _ in range(2):
         scratch += [vmem(2 * GIVE[l][1], LEV[l].rows, 128) for l in range(6)]
-    scratch += [vmem(*LEV[0].shape())]
+    scratch += [vmem(*LEV[0].shape())] * 2
     scratch += [vmem(2, 64, 128)] * 2 + [vmem(2, 80, 128)] * 2 + [vmem(32, 8, 128)] * 4
     scratch += [vmem(32, 32, 128), vmem(16, 16, 128)]
     scratch += [vmem(8, 32, 128), vmem(2, 16, 128), vmem(12, 64, 128), vmem(4, 48, 128)]
@@ -784,11 +826,11 @@
         scratch += [vmem(groups + 2, rows, 128)] * 2
     scratch += [vmem(16, 128), vmem(3, 3, 32, 128), vmem(8, 128), vmem(8, 32, 128), vmem(2048, 128)]
     dma = pltpu.SemaphoreType.DMA((len(PHASES),))
-    scratch += [dma, dma, pltpu.SemaphoreType.DMA((2,)), pltpu.SemaphoreType.REGULAR((2,))]
-    level0 = pltpu.VMEM(LEV[0].shape(), F32)
+    scratch += [dma, dma, pltpu.SemaphoreType.DMA((8,)), pltpu.SemaphoreType.REGULAR((2,))]
+    level0, table = pltpu.VMEM(LEV[0].shape(), F32), pltpu.VMEM((4, 2, LEV[0].nr, 128), F32)
     parts = pl.pallas_call(
         kernel,
-        out_shape=(level0,) * 4 + (pltpu.VMEM((4, 2, LEV[0].nr, 128), F32),),
+        out_shape=(level0,) * 3 + (table, table),
         in_specs=[pl.BlockSpec(memory_space=pl.ANY)] * 2,
         out_specs=(pl.BlockSpec(memory_space=pltpu.VMEM),) * 5,
         scratch_shapes=scratch,
@@ -797,10 +839,10 @@
     block = jax.ShapeDtypeStruct(right_side.shape, F32)
     return pl.pallas_call(
         results,
-        grid=(4,),
         out_shape=(block, block),
         in_specs=[pl.BlockSpec(memory_space=pltpu.VMEM)] * 5,
-        out_specs=(pl.BlockSpec((16, 64, 64), lambda i: (i, 0, 0)),) * 2,
+        out_specs=(pl.BlockSpec(memory_space=pl.ANY),) * 2,
+        scratch_shapes=[vmem(*LEV[0].shape())] * 2 + [vmem(64, 64, 64)] * 2 + [pltpu.SemaphoreType.DMA((2 * len(PARTS),))],
         compiler_params=pltpu.CompilerParams(vmem_limit_bytes=12 * 2**20),
     )(*parts)
 

time: 58.8 us -> 56.3 us (0.957)
  Pallas kernels: 58 us -> 55.4 us
    pallas_call x2, Pallas kernels: 58 us -> 55.4 us  [the longest x1 53 us: per_device(): pl.pallas_call(kernel, out_shape=(level0,) * 3 + (table, table), in_specs...]
where the time goes in v4:
time: 56.3 us; the launch traced here: 56.2 us
  Pallas kernels  55.4 us (98%)
  between operations  0.8 us (1%)
    pallas_call x1, Pallas kernels, per_device(): pl.pallas_call(kernel, out_shape=(level0,) * 3 + (table, table), in_specs...  53 us
    pallas_call x1, Pallas kernels, per_device(): pl.pallas_call(results, out_shape=(block, block), in_specs=[pl.BlockSpec(...  2.42 us

profile of v4, /device:TPU:1, one launch (start us, length us, event | category | flops | bytes accessed | tf_op | source)
XLA Modules:
  0.0 56.2 jit_solution(447431256734782354)
XLA Ops:
  0.6 53.0 %shard_map.41 = (f32[38,80,128]{2,1,0:T(8,128)S(1)}, f32[38,80,128]{2,1,0:T(8,128)S(1)}, f32[38,80,128]{2,1,0:T(8,128)S(1)}, f32[4,2,72,128]{3,2,1,0:T(8,128)S(1)}, f32[4,2,72,128]{3,2,1,0:T(8,128)S(1)}) custom-call(f32[64,64,64]{2,1,0:T(8,128)} %refs_0_.1, f32[64,64,64]{2,1,0:T(8,128)} %refs_1_.1), custom_call_target="tpu_custom_call" | custom-call | tf_op jit(solution)/shard_map/pallas_call | solution.py:831
  53.6 2.4 %shard_map.42 = (f32[64,64,64]{2,1,0:T(8,128)}, f32[64,64,64]{2,1,0:T(8,128)}) custom-call(f32[38,80,128]{2,1,0:T(8,128)S(1)} %get-tuple-element.7.R, f32[38,80,128]{2,1,0:T(8,128)S(1)} %get-tuple-element.8.FR, f32[38,80,128]{2,1,0:T(8,128)S(1)} %get-tuple-element.9.FB, f32[4,2,72,128]{3,2,1,0:T(8,128)S(1)} %get-tuple-element.10.C, ...), custom_call_target="tpu_custom_call" | custom-call | tf_op jit(solution)/shard_map/pallas_call | solution.py:840

commit v5 on v4

--- a/solution.py
+++ b/solution.py
@@ -38,7 +38,8 @@
 BLACK_DOWN = {0: (2, 34, 4, 72), 1: (2, 22, 8, 48), 2: (2, 14, 8, 32), 3: (2, 10, 8, 24), **ALL}
 BLACK_UP = {1: (3, 20, 12, 40), 2: (3, 12, 12, 24), 3: (3, 8, 12, 16), **ALL}
 CORRECTED = {0: (1, 36, 4, 72), 1: (2, 22, 8, 48), 2: (2, 14, 8, 32), 3: (2, 10, 8, 24), **ALL}
-PHASES = ("f", "v", 1, 2, "3", "4")
+PHASES = ("f", "v", 1, 2, "3", "4", "fz", "1z", "2z")
+BESIDE = [(0, 0, -1), (0, 0, 1)]
 WIDTH = {1: 6, 2: 7}
 
 
@@ -130,13 +131,13 @@
     me = (gx, gy, gz)
 
     def fetch(c):
-        cut = pl.ds(32 * c, 32)
+        cut = pl.ds(2 * FETCHED[c], 2 * (FETCHED[c + 1] - FETCHED[c]))
         return [
             pltpu.make_async_copy(src.at[cut], dst.at[cut], in_sem.at[2 * c + i])
             for i, (src, dst) in enumerate(((u_hbm, u_in), (f_hbm, f_in)))
         ]
 
-    for c in range(2):
+    for c in range(len(FETCHED) - 1):
         for copy in fetch(c):
             copy.start()
 
@@ -208,14 +209,14 @@
             out[0][i0 // 16] = lo
             out[1][i0 // 16] = hi
 
-    for c in range(2):
+    for c, (start, end) in enumerate(zip(FETCHED, FETCHED[1:])):
         for copy in fetch(c):
             copy.wait()
-        for p in range(3 + 16 * c, 19 + 16 * c):
+        for p in range(3 + start, 3 + end):
             apart(p)
-        for p in range(3 + 16 * c, 19 + 16 * c):
+        for p in range(3 + start, 3 + end):
             faces_of(p)
-        pack_faces(lambda i: T[3 + i, 8:72, :], zs["f"], 16, 0, 61, 8, 0, 16 * c)
+        pack_faces(lambda i: T[3 + i, 8:72, :], zs["f"], end - start, 0, 61, 8, 0, start)
     for side, (near, next_) in enumerate(((3, 4), (34, 33))):
         for k, (a, other) in enumerate(((near, FR[0]), (next_, FB[0]))):
             xs[side][k] = pick(lane < 64, B[0][a, 8:72, :], turn(other[near, 8:72, :], 64))
@@ -268,8 +269,8 @@
 
         return pieces
 
-    def exchange(key, arrays, oy, n, hz):
-        packed = halo(key, ACROSS, faces(key, oy, n, hz))
+    def exchange(key, arrays, oy, n, hz, directions):
+        packed = halo(key, directions, faces(key, oy, n, hz))
         return both(packed, halo(key, FLAT, sides(arrays, oy, n)))
 
     def settle(what, arrived, left):
@@ -299,7 +300,8 @@
         side = 0 if d[1] < 0 else 1
         return [(ys[side].at[:, pl.ds(0, 3), :], yr[1 - side].at[:, pl.ds(0, 3), :], 96)]
 
-    first = halo("f", ACROSS, faces("f", 8, 64, 3))
+    beside0 = halo("fz", BESIDE, faces("f", 8, 64, 3))
+    first = halo("f", FAR, faces("f", 8, 64, 3))
     first = both(first, halo("f", FLAT, lambda d: first_sides(d) if d[0] else first_rows(d)))
     def outside(ref, po, own, hp, oy, n, hr):
         planes, rows = ref.shape[0], ref.shape[1]
@@ -414,9 +416,6 @@
             return jnp.where(x == 0, 1, jnp.where(x == lv.total - 2, 2, 0))
         return jnp.where(x == 0, 1, jnp.where(x == lv.total - 2, 2, jnp.where((x < 0) | (x >= lv.total), 3, 0)))
 
-    settle(first, True, True)
-    tokens(0, 2, True)
-
     def slot_of(i, n):
         groups = n // 16
         if i < 0:
@@ -425,12 +424,22 @@
             return groups + 1, i - n
         return 1 + i // 16, i % 16
 
-    def unpack_first(i):
+    def unpack_first(i, r0, nr, which):
         g, j = slot_of(i, 32)
-        low, high = zr["f"][0][g, 4:76, :], zr["f"][1][g, 4:76, :]
-        for ref, at, width, shift in ((B[0], 0, 3, 64), (FR[0], 3, 2, 61), (FB[0], 5, 1, 59)):
+        rows = pl.ds(r0, nr)
+        low, high = zr["f"][0][g, rows, :], zr["f"][1][g, rows, :]
+        for k, at, width, shift in which:
+            ref = (B, FR, FB)[k][0]
             w = turn(pick(within(8 * j + at, width), high, low), shift - 8 * j)
-            ref[3 + i, 4:76, :] = pick(lane < 64, ref[3 + i, 4:76, :], w)
+            ref[3 + i, rows, :] = pick(lane < 64, ref[3 + i, rows, :], w)
+
+    settle(beside0, True, False)
+    for i in range(32):
+        unpack_first(i, 8, 64, LANE_FACES)
+
+    settle(first, True, True)
+    settle(beside0, False, True)
+    tokens(0, 2, True)
 
     for side, (near, next_) in enumerate(((2, 1), (35, 36))):
         rows = pl.ds(4, 72)
@@ -439,6 +448,8 @@
         B[0][next_, rows, :] = b
         FR[0][near, rows, :] = turn(a, 64)
         FB[0][near, rows, :] = turn(b, 64)
+    for i in (-2, -1, 32, 33):
+        unpack_first(i, 4, 72, LANE_FACES[: 3 if -1 <= i < 33 else 1])
     for i in range(32):
         for side, (rb, rr, rk) in enumerate(((5, 6, 7), (72, 72, 72))):
             t = yr[side][i]
@@ -446,8 +457,7 @@
             B[0][3 + i, rb : rb + 3, :] = t[0:3]
             FR[0][3 + i, rr : rr + 2, :] = f[0:2]
             FB[0][3 + i, rk : rk + 1, :] = f[2:3]
-    for i in range(-2, 34):
-        unpack_first(i)
+            unpack_first(i, (0, 72)[side], 8, LANE_FACES)
 
     def red_sweep(l):
         lv = LEV[l]
@@ -519,7 +529,17 @@
             PS[l][q] = t
         pack_faces(lambda i: G[l][i], zs[l], n, 0, n - 8, 8, 128 - 2 * n)
         wide = 8 // per
-        return exchange(l, [(PS[l], 0, PR[l], wide, n // per, wide, w)], 16, n, w)
+        beside = halo(f"{l}z", BESIDE, faces(l, 16, n, w))
+        return beside, exchange(l, [(PS[l], 0, PR[l], wide, n // per, wide, w)], 16, n, w, FAR)
+
+    def side_lanes(l, i, rows):
+        g, j = slot_of(i, LEV[l].n)
+        return turn(pick(within(8 * j, 8), zr[l][1][g, rows, :], zr[l][0][g, rows, :]), LEV[l].n - 8 * j)
+
+    def own_side_lanes(l):
+        n = LEV[l].n
+        for i in range(n):
+            G[l][i] = pick(lane < n, G[l][i], side_lanes(l, i, pl.ds(16, n)))
 
     def split_right_side(l):
         lv = LEV[l]
@@ -527,18 +547,18 @@
         per = 128 // n
 
         def natural(i):
-            g, j = slot_of(i, n)
-            rows = pl.ds(lv.r0, lv.nr)
-            side = pick(within(8 * j, 8), zr[l][1][g, rows, :], zr[l][0][g, rows, :])
             q, k = (i + 8) // per, (i + 8) % per
+
+            def tile(r, nr):
+                rows = pl.ds(r, nr)
+                return pick(lane < n, turn(PR[l][q, rows, :], -n * k), side_lanes(l, i, rows))
+
             if 0 <= i < n:
-                below, above = (turn(PR[l][q, pl.ds(r, 8), :], -n * k) for r in (8, 16 + n))
-                here = jnp.concatenate([below, G[l][i], above], axis=0)
-            else:
-                here = turn(PR[l][q, rows, :], -n * k)
-            return pick(lane < n, here, turn(side, n - 8 * j))
-
-        for p in range(lv.p0, lv.p0 + lv.np):
+                return jnp.concatenate([tile(8, 8), G[l][i], tile(16 + n, 8)], axis=0)
+            return tile(lv.r0, lv.nr)
+
+        p0, count, _, _ = BLACK_DOWN[l] if l == 1 else (lv.p0, lv.np, 0, 0)
+        for p in range(p0, p0 + count):
             a, b = natural(2 * (p - lv.po)), natural(2 * (p - lv.po) + 1)
             store_colours(l, p, a, b)
 
@@ -550,7 +570,7 @@
         FB[l][p, rows, :] = pick(m, a, b)
         R[l][p, rows, :] = red * C[l][kind(l, p), 0]
 
-    second = send_right_side(1)
+    beside1, second = send_right_side(1)
     def keep_black(p):
         H[p, 8:72, :] = B[0][p, 8:72, :]
 
@@ -558,14 +578,18 @@
 
     tokens(0, 2, False)
     tokens(1, 4, True)
+    settle(beside1, True, False)
+    own_side_lanes(1)
     settle(second, True, False)
     split_right_side(1)
     black_sweep(1, BLACK_DOWN, True)
     residual(1)
     restrict_to(1, G[2], 0, 0)
-    third = send_right_side(2)
+    beside2, third = send_right_side(2)
     pack_faces(lambda i: B[0][3 + i, 8:72, :], zs["v"], 32, 0, 61, 3, 0)
-    kept = exchange("v", [(B[0], 3, H, 3, 32, 2, 3)], 8, 64, 3)
+    kept = exchange("v", [(B[0], 3, H, 3, 32, 2, 3)], 8, 64, 3, ACROSS)
+    settle(beside2, True, False)
+    own_side_lanes(2)
     settle(third, True, False)
     split_right_side(2)
     black_sweep(2, BLACK_DOWN, True)
@@ -732,7 +756,7 @@
     expand(0)
     correct(0)
     red_sweep(0)
-    for what in (second, third, (k3, blocks), plane):
+    for what in (beside1, second, beside2, third, (k3, blocks), plane):
         settle(what, False, True)
 
 
@@ -781,10 +805,13 @@
 
 
 PARTS = (4, 4, 4, 4, 4, 4, 4, 4)
+LANE_FACES = ((0, 0, 3, 64), (1, 3, 2, 61), (2, 5, 1, 59))
+FETCHED = (0, 8, 16, 24, 32)
 EDGES = tuple(itertools.product((False, True), repeat=3))
 AROUND = sorted((d for d in itertools.product((-1, 0, 1), repeat=3) if any(d)), key=lambda d: -sum(map(abs, d)))
 FLAT = [d for d in AROUND if d[2] == 0]
 ACROSS = [d for d in AROUND if d[2]]
+FAR = [d for d in ACROSS if d not in BESIDE]
 EDGE = {0: -1, 1: -1, 2: -1, 3: -1, 4: 2, 5: -1}
 
 

time: 56.3 us -> 55.6 us (0.988)
  Pallas kernels: 55.4 us -> 54.7 us
    pallas_call x1, Pallas kernels: 53 us -> 52.3 us  [per_device(): pl.pallas_call(kernel, out_shape=(level0,) * 3 + (table, table), in_specs...]
where the time goes in v5:
time: 55.6 us; the launch traced here: 55.5 us
  Pallas kernels  54.7 us (98%)
  between operations  0.8 us (1%)
    pallas_call x1, Pallas kernels, per_device(): pl.pallas_call(kernel, out_shape=(level0,) * 3 + (table, table), in_specs...  52.3 us
    pallas_call x1, Pallas kernels, per_device(): pl.pallas_call(results, out_shape=(block, block), in_specs=[pl.BlockSpec(...  2.42 us

profile of v5, /device:TPU:1, one launch (start us, length us, event | category | flops | bytes accessed | tf_op | source)
XLA Modules:
  0.0 55.5 jit_solution(4900760760582966541)
XLA Ops:
  0.6 52.3 %shard_map.41 = (f32[38,80,128]{2,1,0:T(8,128)S(1)}, f32[38,80,128]{2,1,0:T(8,128)S(1)}, f32[38,80,128]{2,1,0:T(8,128)S(1)}, f32[4,2,72,128]{3,2,1,0:T(8,128)S(1)}, f32[4,2,72,128]{3,2,1,0:T(8,128)S(1)}) custom-call(f32[64,64,64]{2,1,0:T(8,128)} %refs_0_.1, f32[64,64,64]{2,1,0:T(8,128)} %refs_1_.1), custom_call_target="tpu_custom_call" | custom-call | tf_op jit(solution)/shard_map/pallas_call | solution.py:858
  52.9 2.4 %shard_map.42 = (f32[64,64,64]{2,1,0:T(8,128)}, f32[64,64,64]{2,1,0:T(8,128)}) custom-call(f32[38,80,128]{2,1,0:T(8,128)S(1)} %get-tuple-element.7.R, f32[38,80,128]{2,1,0:T(8,128)S(1)} %get-tuple-element.8.FR, f32[38,80,128]{2,1,0:T(8,128)S(1)} %get-tuple-element.9.FB, f32[4,2,72,128]{3,2,1,0:T(8,128)S(1)} %get-tuple-element.10.C, ...), custom_call_target="tpu_custom_call" | custom-call | tf_op jit(solution)/shard_map/pallas_call | solution.py:867

commit v6 on v5

--- a/solution.py
+++ b/solution.py
@@ -92,6 +92,15 @@
         return carry
 
     lax.fori_loop(0, count // step, some, 0)
+
+
+def emit(*stages):
+    start = min(first + lag for first, _, lag, _ in stages)
+    end = max(first + count + lag for first, count, lag, _ in stages)
+    for t in range(start, end):
+        for first, count, lag, body in stages:
+            if first <= t - lag < first + count:
+                body(t - lag)
 
 
 def around(src, p, r0, nr, up):
@@ -459,7 +468,7 @@
             FB[0][3 + i, rk : rk + 1, :] = f[2:3]
             unpack_first(i, (0, 72)[side], 8, LANE_FACES)
 
-    def red_sweep(l):
+    def red(l, lag):
         lv = LEV[l]
         p0, count, r0, nr = RED[l]
         rows, table = pl.ds(r0, nr), pl.ds(r0 - lv.r0, nr)
@@ -467,9 +476,9 @@
         def body(p):
             R[l][p, rows, :] = (FR[l][p, rows, :] + around(B[l], p, r0, nr, m)) * C[l][kind(l, p), 0, table, :]
 
-        sweep_loop(p0, count, 36, body)
-
-    def black_sweep(l, region, keep):
+        return p0, count, lag, body
+
+    def black(l, region, keep, lag):
         lv = LEV[l]
         p0, count, r0, nr = region[l]
         rows, table = pl.ds(r0, nr), pl.ds(r0 - lv.r0, nr)
@@ -482,7 +491,13 @@
             if keep:
                 T[p, rows, :] = fs - D[l][t, 1, table, :] * b
 
-        sweep_loop(p0, count, 36, body)
+        return p0, count, lag, body
+
+    def red_sweep(l):
+        emit(red(l, 0))
+
+    def black_sweep(l, region, keep):
+        emit(black(l, region, keep, 0))
 
     def red_residual(l, p):
         lv = LEV[l]
@@ -490,13 +505,16 @@
         at = lv.oy - lv.r0
         return FR[l][p, pl.ds(lv.oy, lv.n), :] + s - D[l][kind(l, p), 0, pl.ds(at, lv.n), :] * R[l][p, pl.ds(lv.oy, lv.n), :]
 
-    def residual(l):
+    def residue(l, lag):
         lv = LEV[l]
 
         def body(p):
             T[p, pl.ds(lv.oy, lv.n), :] = T[p, pl.ds(lv.oy, lv.n), :] + red_residual(l, p)
 
-        sweep_loop(lv.po, lv.n // 2, 32, body)
+        return lv.po, lv.n // 2, lag, body
+
+    def residual(l):
+        emit(residue(l, 0))
 
     def coarse_side(l, p):
         lv = LEV[l]
@@ -505,19 +523,14 @@
         z = 2 * lane_index(half)
         return 0.5 * (take(u, z & 127) + take(u, (z + 1) & 127))
 
-    red_sweep(0)
-    black_sweep(0, BLACK_DOWN, True)
-
-    def restrict_to(l, dst, first_plane, first_row):
+    def restrict(l, dst, lag):
         lv = LEV[l]
 
         def body(p):
-            dst[p - lv.po + first_plane, pl.ds(first_row, lv.n // 2), :] = coarse_side(l, p)
-
-        sweep_loop(lv.po, lv.n // 2, 32, body)
-
-    residual(0)
-    restrict_to(0, G[1], 0, 0)
+            dst[p - lv.po, pl.ds(0, lv.n // 2), :] = coarse_side(l, p)
+
+        return lv.po, lv.n // 2, lag, body
+
 
     def send_right_side(l):
         n, w = LEV[l].n, WIDTH[l]
@@ -570,6 +583,7 @@
         FB[l][p, rows, :] = pick(m, a, b)
         R[l][p, rows, :] = red * C[l][kind(l, p), 0]
 
+    emit(red(0, 0), black(0, BLACK_DOWN, True, 8), residue(0, 16), restrict(0, G[1], 22))
     beside1, second = send_right_side(1)
     def keep_black(p):
         H[p, 8:72, :] = B[0][p, 8:72, :]
@@ -584,7 +598,7 @@
     split_right_side(1)
     black_sweep(1, BLACK_DOWN, True)
     residual(1)
-    restrict_to(1, G[2], 0, 0)
+    emit(restrict(1, G[2], 0))
     beside2, third = send_right_side(2)
     pack_faces(lambda i: B[0][3 + i, 8:72, :], zs["v"], 32, 0, 61, 3, 0)
     kept = exchange("v", [(B[0], 3, H, 3, 32, 2, 3)], 8, 64, 3, ACROSS)
@@ -679,7 +693,7 @@
     for l in (4, 5):
         black_sweep(l, BLACK_DOWN, True)
         residual(l)
-        restrict_to(l, N[l + 1], 0, 0)
+        emit(restrict(l, N[l + 1], 0))
         lv = LEV[l + 1]
         for p in range(lv.p0, lv.p0 + lv.np):
             store_colours(l + 1, p, N[l + 1][2 * (p - 1)], N[l + 1][2 * (p - 1) + 1])
@@ -688,7 +702,7 @@
         red_sweep(6)
         black_sweep(6, BLACK_UP, False)
 
-    def expand(l):
+    def expanding(l, lag):
         lf, lc = LEV[l], LEV[l + 1]
         c0, cn, r0, rn = GIVE[l]
         fine0 = lf.oy + 2 * (r0 - lc.oy)
@@ -713,9 +727,12 @@
                     EX[l][2 * i + a, pl.ds(fine0 + k, rn, stride=2), :] = here
                     EZ[l][2 * i + a, pl.ds(fine0 + k, rn, stride=2), :] = there
 
-        sweep_loop(0, cn, 20, body)
-
-    def correct(l):
+        return EDGE[l], 2 * cn, lag, lambda p: body((p - EDGE[l]) // 2) if (p - EDGE[l]) % 2 == 0 else None
+
+    def expand(l):
+        emit(expanding(l, 0))
+
+    def correcting(l, lag):
         lv = LEV[l]
         second_row = (iota((8, 128), 0) & 1) == 1
         p0, count, r0, nr = CORRECTED[l]
@@ -734,7 +751,10 @@
         def plain(p):
             B[l][p, rows, :] = start[p, rows, :] + body(p)
 
-        sweep_loop(p0, count, 36, plain)
+        return p0, count, lag, plain
+
+    def correct(l):
+        emit(correcting(l, 0))
 
     for l in (5, 4):
         expand(l)
@@ -749,13 +769,8 @@
     correct(2)
     red_sweep(2)
     black_sweep(2, BLACK_UP, False)
-    expand(1)
-    correct(1)
-    red_sweep(1)
-    black_sweep(1, BLACK_UP, False)
-    expand(0)
-    correct(0)
-    red_sweep(0)
+    emit(expanding(1, 0), correcting(1, 8), red(1, 12), black(1, BLACK_UP, False, 18))
+    emit(expanding(0, 0), correcting(0, 12), red(0, 16))
     for what in (beside1, second, beside2, third, (k3, blocks), plane):
         settle(what, False, True)
 
@@ -776,35 +791,44 @@
         B[p, 4:76, :] = b
         T[p, 4:76, :] = fs - D[t, 1] * b
 
-    def finish(p):
-        x = 2 * (p - lv.po)
-        r, b = R[p, 8:72, :], B[p, 8:72, :]
-        u_out[x] = pick(m, b, r)[:, 0:64]
-        u_out[x + 1] = pick(m, r, b)[:, 0:64]
-        left = FR[p, 8:72, :] + around(B, p, lv.oy, lv.n, m) - D[kind(p), 0, 4:68, :] * r
-        b = T[p, 8:72, :]
-        r_out[x] = pick(m, b, left)[:, 0:64]
-        r_out[x + 1] = pick(m, left, b)[:, 0:64]
-
-    done, first, copies = 2, 3, []
-    for part in PARTS:
-        ready = min(first + part + (PARTS[0] if first == 3 else part), 35)
-        for p in range(done, ready + 1):
+    copies = []
+
+    def out(src, dst, k):
+        cut = pl.ds(2 * (STARTS[k] - 3), 2 * PARTS[k])
+        copy = pltpu.make_async_copy(src.at[cut], dst.at[cut], sem.at[len(copies)])
+        copy.start()
+        copies.append(copy)
+
+    def solve(k):
+        for p in range(STARTS[k] + (1 if k else -1), STARTS[k] + PARTS[k] + 1):
             black(p)
-        done = ready + 1
-        for p in range(first, first + part):
-            finish(p)
-        cut = pl.ds(2 * (first - 3), 2 * part)
-        for src, dst in ((u_out, u_hbm), (r_out, r_hbm)):
-            copy = pltpu.make_async_copy(src.at[cut], dst.at[cut], sem.at[len(copies)])
-            copy.start()
-            copies.append(copy)
-        first += part
+        for p in range(STARTS[k], STARTS[k] + PARTS[k]):
+            x = 2 * (p - lv.po)
+            r, b = R[p, 8:72, :], B[p, 8:72, :]
+            u_out[x] = pick(m, b, r)[:, 0:64]
+            u_out[x + 1] = pick(m, r, b)[:, 0:64]
+        out(u_out, u_hbm, k)
+
+    def remain(k):
+        for p in range(STARTS[k], STARTS[k] + PARTS[k]):
+            x = 2 * (p - lv.po)
+            left = FR[p, 8:72, :] + around(B, p, lv.oy, lv.n, m) - D[kind(p), 0, 4:68, :] * R[p, 8:72, :]
+            b = T[p, 8:72, :]
+            r_out[x] = pick(m, b, left)[:, 0:64]
+            r_out[x + 1] = pick(m, left, b)[:, 0:64]
+        out(r_out, r_hbm, k)
+
+    solve(0)
+    for k in range(1, len(PARTS)):
+        solve(k)
+        remain(k - 1)
+    remain(len(PARTS) - 1)
     for copy in copies:
         copy.wait()
 
 
 PARTS = (4, 4, 4, 4, 4, 4, 4, 4)
+STARTS = tuple(3 + sum(PARTS[:k]) for k in range(len(PARTS)))
 LANE_FACES = ((0, 0, 3, 64), (1, 3, 2, 61), (2, 5, 1, 59))
 FETCHED = (0, 8, 16, 24, 32)
 EDGES = tuple(itertools.product((False, True), repeat=3))

time: 55.6 us -> 55.7 us (level)
  no operation moved by 1% of the time
where the time goes in v6:
time: 55.7 us; the launch traced here: 55.6 us
  Pallas kernels  54.8 us (98%)
  between operations  0.8 us (1%)
    pallas_call x1, Pallas kernels, per_device(): pl.pallas_call(kernel, out_shape=(level0,) * 3 + (table, table), in_specs...  52.4 us
    pallas_call x1, Pallas kernels, per_device(): pl.pallas_call(results, out_shape=(block, block), in_specs=[pl.BlockSpec(...  2.34 us

profile of v6, /device:TPU:1, one launch (start us, length us, event | category | flops | bytes accessed | tf_op | source)
XLA Modules:
  0.0 55.6 jit_solution(16570108649695218105)
XLA Ops:
  0.6 52.4 %shard_map.41 = (f32[38,80,128]{2,1,0:T(8,128)S(1)}, f32[38,80,128]{2,1,0:T(8,128)S(1)}, f32[38,80,128]{2,1,0:T(8,128)S(1)}, f32[4,2,72,128]{3,2,1,0:T(8,128)S(1)}, f32[4,2,72,128]{3,2,1,0:T(8,128)S(1)}) custom-call(f32[64,64,64]{2,1,0:T(8,128)} %refs_0_.1, f32[64,64,64]{2,1,0:T(8,128)} %refs_1_.1), custom_call_target="tpu_custom_call" | custom-call | tf_op jit(solution)/shard_map/pallas_call | solution.py:882
  53.1 2.3 %shard_map.42 = (f32[64,64,64]{2,1,0:T(8,128)}, f32[64,64,64]{2,1,0:T(8,128)}) custom-call(f32[38,80,128]{2,1,0:T(8,128)S(1)} %get-tuple-element.7.R, f32[38,80,128]{2,1,0:T(8,128)S(1)} %get-tuple-element.8.FR, f32[38,80,128]{2,1,0:T(8,128)S(1)} %get-tuple-element.9.FB, f32[4,2,72,128]{3,2,1,0:T(8,128)S(1)} %get-tuple-element.10.C, ...), custom_call_target="tpu_custom_call" | custom-call | tf_op jit(solution)/shard_map/pallas_call | solution.py:891

commit v7 on v5

--- a/solution.py
+++ b/solution.py
@@ -776,35 +776,44 @@
         B[p, 4:76, :] = b
         T[p, 4:76, :] = fs - D[t, 1] * b
 
-    def finish(p):
-        x = 2 * (p - lv.po)
-        r, b = R[p, 8:72, :], B[p, 8:72, :]
-        u_out[x] = pick(m, b, r)[:, 0:64]
-        u_out[x + 1] = pick(m, r, b)[:, 0:64]
-        left = FR[p, 8:72, :] + around(B, p, lv.oy, lv.n, m) - D[kind(p), 0, 4:68, :] * r
-        b = T[p, 8:72, :]
-        r_out[x] = pick(m, b, left)[:, 0:64]
-        r_out[x + 1] = pick(m, left, b)[:, 0:64]
-
-    done, first, copies = 2, 3, []
-    for part in PARTS:
-        ready = min(first + part + (PARTS[0] if first == 3 else part), 35)
-        for p in range(done, ready + 1):
+    copies = []
+
+    def out(src, dst, k):
+        cut = pl.ds(2 * (STARTS[k] - 3), 2 * PARTS[k])
+        copy = pltpu.make_async_copy(src.at[cut], dst.at[cut], sem.at[len(copies)])
+        copy.start()
+        copies.append(copy)
+
+    def solve(k):
+        for p in range(STARTS[k] + (1 if k else -1), STARTS[k] + PARTS[k] + 1):
             black(p)
-        done = ready + 1
-        for p in range(first, first + part):
-            finish(p)
-        cut = pl.ds(2 * (first - 3), 2 * part)
-        for src, dst in ((u_out, u_hbm), (r_out, r_hbm)):
-            copy = pltpu.make_async_copy(src.at[cut], dst.at[cut], sem.at[len(copies)])
-            copy.start()
-            copies.append(copy)
-        first += part
+        for p in range(STARTS[k], STARTS[k] + PARTS[k]):
+            x = 2 * (p - lv.po)
+            r, b = R[p, 8:72, :], B[p, 8:72, :]
+            u_out[x] = pick(m, b, r)[:, 0:64]
+            u_out[x + 1] = pick(m, r, b)[:, 0:64]
+        out(u_out, u_hbm, k)
+
+    def remain(k):
+        for p in range(STARTS[k], STARTS[k] + PARTS[k]):
+            x = 2 * (p - lv.po)
+            left = FR[p, 8:72, :] + around(B, p, lv.oy, lv.n, m) - D[kind(p), 0, 4:68, :] * R[p, 8:72, :]
+            b = T[p, 8:72, :]
+            r_out[x] = pick(m, b, left)[:, 0:64]
+            r_out[x + 1] = pick(m, left, b)[:, 0:64]
+        out(r_out, r_hbm, k)
+
+    solve(0)
+    for k in range(1, len(PARTS)):
+        solve(k)
+        remain(k - 1)
+    remain(len(PARTS) - 1)
     for copy in copies:
         copy.wait()
 
 
 PARTS = (4, 4, 4, 4, 4, 4, 4, 4)
+STARTS = tuple(3 + sum(PARTS[:k]) for k in range(len(PARTS)))
 LANE_FACES = ((0, 0, 3, 64), (1, 3, 2, 61), (2, 5, 1, 59))
 FETCHED = (0, 8, 16, 24, 32)
 EDGES = tuple(itertools.product((False, True), repeat=3))

time: 55.6 us -> 55.6 us (level)
  no operation moved by 1% of the time
where the time goes in v7:
time: 55.6 us; the launch traced here: 55.4 us
  Pallas kernels  54.6 us (98%)
  between operations  0.8 us (1%)
    pallas_call x1, Pallas kernels, per_device(): pl.pallas_call(kernel, out_shape=(level0,) * 3 + (table, table), in_specs...  52.3 us
    pallas_call x1, Pallas kernels, per_device(): pl.pallas_call(results, out_shape=(block, block), in_specs=[pl.BlockSpec(...  2.34 us

profile of v7, /device:TPU:1, one launch (start us, length us, event | category | flops | bytes accessed | tf_op | source)
XLA Modules:
  0.0 55.4 jit_solution(8677215811963725309)
XLA Ops:
  0.6 52.3 %shard_map.41 = (f32[38,80,128]{2,1,0:T(8,128)S(1)}, f32[38,80,128]{2,1,0:T(8,128)S(1)}, f32[38,80,128]{2,1,0:T(8,128)S(1)}, f32[4,2,72,128]{3,2,1,0:T(8,128)S(1)}, f32[4,2,72,128]{3,2,1,0:T(8,128)S(1)}) custom-call(f32[64,64,64]{2,1,0:T(8,128)} %refs_0_.1, f32[64,64,64]{2,1,0:T(8,128)} %refs_1_.1), custom_call_target="tpu_custom_call" | custom-call | tf_op jit(solution)/shard_map/pallas_call | solution.py:867
  52.9 2.3 %shard_map.42 = (f32[64,64,64]{2,1,0:T(8,128)}, f32[64,64,64]{2,1,0:T(8,128)}) custom-call(f32[38,80,128]{2,1,0:T(8,128)S(1)} %get-tuple-element.7.R, f32[38,80,128]{2,1,0:T(8,128)S(1)} %get-tuple-element.8.FR, f32[38,80,128]{2,1,0:T(8,128)S(1)} %get-tuple-element.9.FB, f32[4,2,72,128]{3,2,1,0:T(8,128)S(1)} %get-tuple-element.10.C, ...), custom_call_target="tpu_custom_call" | custom-call | tf_op jit(solution)/shard_map/pallas_call | solution.py:876
